TPU v7x, 32 devices: a whole 2x2x4 slice. The times are simulated.
32 devices in a mesh: groups: 2 (over x), tile: 16 (over z, y, core).
Axes of the slice: x: 2, y: 2, z: 4, core: 2. Of those that a mesh axis runs over, the one named last changes fastest.
Arguments:
- features: bfloat16 [8, 384, 16, 8, 16], P('groups', None, 'tile'), parts along dimension 0, may hold values from -6 to 6
- cache_first: bfloat16 [4, 384, 16, 8, 16], P('groups', None, 'tile'), parts along dimension 0, may hold values from -6 to 6
- cache_second: bfloat16 [4, 192, 16, 16, 32], P('groups', None, 'tile'), parts along dimension 0, may hold values from -6 to 6
- cache_third: bfloat16 [4, 96, 16, 32, 64], P('groups', None, 'tile'), parts along dimension 0, may hold values from -6 to 6
- weight_first: bfloat16 [3, 3, 3, 192, 384], replicated, may hold values from -0.0625 to 0.0625
- weight_second: bfloat16 [3, 3, 3, 96, 192], replicated, may hold values from -0.078125 to 0.078125
- weight_third: bfloat16 [3, 3, 3, 3, 96], replicated, may hold values from -0.125 to 0.125
- gain_first: float32 [384], replicated, may hold values from 0.1 to 1.9
- gain_second: float32 [192], replicated, may hold values from 0.1 to 1.9
- gain_third: float32 [96], replicated, may hold values from 0.1 to 1.9
Outputs:
- pixels: float32 [8, 3, 16, 32, 64], P('groups', None, 'tile'), parts along dimension 0
There are 2 independent parts, one for each index of `groups`. A program takes and returns all parts, laid end to end along the dimension named above; an argument that names none is the same for every part. Nothing has to cross between parts.
All inputs are finite; a program needn't handle non-finite values.
Results may differ from a plain program's by a relative error of at most 0.0085.
Values may be sent and summed in bfloat16 or wider, within the bound.
No kernel may reach another device: no remote copies, remote signals or barrier semaphores. Data moves between devices by JAX's collectives and lax.ppermute only.
A program may use at most 64 MiB of HBM per device.

v0:
```python
import functools

import jax
import jax.numpy as jnp
import numpy as np
from jax import lax
from jax.experimental import pallas as pl
from jax.experimental.pallas import tpu as pltpu
from jax.sharding import PartitionSpec as P

TILES_X = 8
EPS = 1e-06
F32 = jnp.float32
BF16 = jnp.bfloat16
PITCH = 24


def partner(index, size, odd):
    other = index ^ 1 if not odd else ((index - 1) ^ 1) + 1
    return other if 0 <= other < size and (not odd or index > 0) else index


def pairs_of(count, row_pair, col_pair):
    rows = count // TILES_X
    out = []
    for k in range(count):
        m = (k + TILES_X // 2) % count
        r, c = divmod(m, TILES_X)
        r2 = r if row_pair is None else partner(r, rows, row_pair)
        c2 = c if col_pair is None else partner(c, TILES_X, col_pair)
        if (row_pair is not None and r2 == r) or (col_pair is not None and c2 == c):
            r2, c2 = r, c
        out.append((k, (r2 * TILES_X + c2 - TILES_X // 2) % count))
    return out


def swap(values, count, row_pair, col_pair):
    return lax.ppermute(values, "tile", pairs_of(count, row_pair, col_pair))


def edge(values, axis, size, last):
    total = values.shape[axis]
    tail = lax.slice_in_dim(values, total - size, total, axis=axis)
    head = lax.slice_in_dim(values, 0, size, axis=axis)
    return jnp.where(last, tail, head)


def joined(second, third):
    gap = -second.shape[-1] % 128
    rest = -third.shape[-1] % 128
    return jnp.concatenate(
        [
            second,
            jnp.zeros(second.shape[:-1] + (gap,), second.dtype),
            third,
            jnp.zeros(third.shape[:-1] + (rest,), third.dtype),
        ],
        -1,
    )


@functools.lru_cache
def fine_taps(rgb):
    slots = np.zeros((2, 4, 3, 4, 4, 4, 2, 3, 3, 3, rgb), np.float32)
    for a in range(4):
        for d in range(3):
            row = (a + d - 1) // 2
            rs, half = {-1: (0, 1), 0: (0, 0), 1: (1, 1), 2: (1, 0)}[row]
            for b in range(4):
                for e in range(3):
                    cs = (b + e - 1) // 2 + 1
                    for t in range(3):
                        for c in range(rgb):
                            slots[rs, cs, 2 - t, b, c, a, half, t, d, e, c] += 1
    flat = slots.reshape(8 * 192, 2, 27 * rgb)
    return np.pad(flat, ((0, 0), (0, 0), (0, 96 - 27 * rgb))).reshape(8 * 192, 192)


@functools.lru_cache
def cache_taps(rgb):
    slots = np.zeros((6, 6, 2, 4, 4, 4, 3, 3, 3, rgb), np.float32)
    for a in range(4):
        for d in range(3):
            for b in range(4):
                for e in range(3):
                    for t in range(2):
                        for c in range(rgb):
                            slots[a + d, b + e, 1 - t, b, c, a, t, d, e, c] += 1
    flat = slots.reshape(36 * 128, 27 * rgb)
    return np.pad(flat, ((0, 0), (0, 96 - 27 * rgb)))


@functools.lru_cache
def spread(height, width):
    out = np.zeros((4, height, width, height, width, 4), np.float32)
    for b in range(4):
        for r in range(height):
            for c in range(width):
                out[b, r, c, r, c, b] = 1
    return out.reshape(4 * height * width, 4 * height * width)


def dot_nt(lhs, rhs):
    return lax.dot_general(lhs, rhs, (((1,), (1,)), ((), ())), preferred_element_type=F32)


def sides(flags):
    top, bottom, left, right, odd = (flags[i] for i in range(5))
    as_f = lambda v: v.astype(F32)
    return (
        as_f(top),
        as_f(bottom),
        (as_f(left * odd), as_f(left * (1 - odd))),
        (as_f(right * (1 - odd)), as_f(right * odd)),
    )


def history_kernel(
    flags, second, third, up2, down2, a2, b2, dau, dbu, dad, dbd, w2, w3, taps3, taps3c,
    part2, part3, wc2, wc3,
    e_lo, e_hi, e3, xc2, xc3, w3c,
):
    top, bottom, left, right = sides(flags)
    frames, tall, wide, chans = second.shape
    c3 = third.shape[-1]
    lo = 128
    hi = chans - lo
    read = lambda ref, *ix: ref[ix].astype(F32)

    w3c[...] = jnp.dot(taps3c[...], w3[0:96, 0:128], preferred_element_type=F32).astype(BF16)
    wc3[...] = jnp.dot(taps3[...], w3[96:288, :], preferred_element_type=F32).astype(BF16)
    for t in range(3):
        rows = {}
        for e in range(3):
            w = [w2[t, d, e].astype(F32) for d in range(3)]
            rows[e] = (w[0], w[0] + w[1], w[1] + w[2], w[2])
        for q in range(2):
            for cs in range(2):
                cols = [
                    rows[0][v] if (q, cs) == (0, 0) else rows[2][v] if (q, cs) == (1, 1)
                    else rows[1][v] + (rows[2][v] if q == 0 else rows[0][v])
                    for v in range(4)
                ]
                for rs in range(2):
                    base = ((t * 2 + q) * 2 + rs) * 2 + cs
                    wc2[base, 0:c3, :] = cols[2 * rs].astype(BF16)
                    wc2[base, c3:2 * c3, :] = cols[2 * rs + 1].astype(BF16)

    off = 8
    def put2(f, row, col, value):
        n = value.shape[0]
        e_lo[f, row, col:col + n, :] = value[:, :lo]
        e_hi[f, row, col:col + n, 0:hi] = value[:, lo:chans]
    for f in range(frames):
        for r in range(tall + 4):
            if r < 2:
                own = read(up2, f, r) * top
                pa, pb, s = read(dau, f, r), read(dbu, f, r), top
            elif r < tall + 2:
                own = read(second, f, r - 2)
                pa, pb, s = read(a2, f, r - 2), read(b2, f, r - 2), 1.0
            else:
                own = read(down2, f, r - tall - 2) * bottom
                pa, pb, s = read(dad, f, r - tall - 2), read(dbd, f, r - tall - 2), bottom
            put2(f, r, off, own)
            put2(f, r, off - 2, pa * (left[0] * s) + pb * (left[1] * s))
            put2(f, r, off + wide, pa * (right[0] * s) + pb * (right[1] * s))
    for k in range(4):
        for f in range(frames):
            for r in range(tall + 4):
                cols = pl.ds(off - 3 + k, PITCH, stride=2)
                xc2[k, f, r, :, 0:lo] = e_lo[f, r, cols, :].astype(BF16)
                xc2[k, f, r, :, lo:chans] = e_hi[f, r, cols, :].astype(BF16)[:, :hi]
    rows_out = tall + 2
    for q in range(2):
        acc = None
        for d in range(3):
            for e in range(3):
                lhs = xc2[e + q, :, d:d + rows_out].reshape(frames * rows_out * PITCH, chans)
                rhs = jnp.concatenate([w2[1, d, e], w2[0, d, e]], 0)
                term = dot_nt(lhs, rhs)
                acc = term if acc is None else acc + term
        acc = acc.reshape(frames, rows_out // 2, 2, PITCH, 2 * c3)
        v0 = acc[0, ..., c3:] + acc[1, ..., :c3]
        v1 = acc[1, ..., c3:]
        for o, v in enumerate((v0, v1)):
            part2[q, o] = jnp.concatenate([v[:, 1], v[:, 0]], -1)

    tall3, wide3 = third.shape[1:3]
    shift = 2 * 128
    def put3(f, row, col, value):
        n = value.shape[0]
        e3[f, row, col:col + n, 0:c3] = value
    for f in range(frames):
        for r in range(tall3):
            put3(f, r + 1, off, read(third, f, r))
        for j in range(2):
            half = wide3 // 2
            put3(f, 0, off + j * half, read(up2, f, j)[:, shift:shift + c3] * top)
            put3(f, tall3 + 1, off + j * half, read(down2, f, j)[:, shift:shift + c3] * bottom)
        for r in range(tall3 // 2):
            pa = read(a2, f, r)[:, shift:shift + c3]
            pb = read(b2, f, r)[:, shift:shift + c3]
            vl = pa * left[0] + pb * left[1]
            vr = pa * right[0] + pb * right[1]
            for j in range(2):
                put3(f, 1 + 2 * r + j, off - 1, vl[j:j + 1])
                put3(f, 1 + 2 * r + j, off + wide3, vr[j:j + 1])
        for row, da, db, s in ((0, dau, dbu, top), (tall3 + 1, dad, dbd, bottom)):
            pa = read(da, f, 0)[0:1, shift:shift + c3]
            pb = read(db, f, 0)[0:1, shift:shift + c3]
            put3(f, row, off - 1, pa * (left[0] * s) + pb * (left[1] * s))
            put3(f, row, off + wide3, pa * (right[0] * s) + pb * (right[1] * s))
    height, width = tall3 // 4, wide3 // 4
    lanes = lax.broadcasted_iota(jnp.int32, (width, 128), 1)
    for k in range(6):
        for f in range(frames):
            for r in range(tall3 + 2):
                value = e3[f, r, pl.ds(off - 1 + k, width, stride=4), :]
                xc3[k, f, r // 4, r % 4] = jnp.where(lanes < c3, value, 0.0).astype(BF16)
    acc = None
    for j in range(6):
        for k in range(0, 6, 2):
            lhs = jnp.concatenate(
                [
                    xc3[kk, :, j // 4:j // 4 + height, j % 4].reshape(frames * height * width, 128)
                    for kk in (k, k + 1)
                ],
                -1,
            )
            base = (j * 6 + k) * 128
            rhs = jnp.concatenate([w3c[base:base + 128], w3c[base + 128:base + 256]], -1)
            term = dot_nt(lhs, rhs)
            acc = term if acc is None else acc + term
    size = height * width
    part3[0] = acc[:size, 64:] + acc[size:, :64]
    part3[1] = acc[size:, 64:]


def normed(values, gain, total):
    meansq = jnp.sum(values * values, axis=-1, keepdims=True) * (1.0 / total)
    out = values * lax.rsqrt(meansq + EPS) * gain
    return out / (1.0 + jnp.exp(-out))


def frames_kernel(
    flags, feats, cache, up1, down1, a1, b1, dau, dbu, dad, dbd, w1, g1, g2, g3,
    part2, part3, wc2, wc3, spread_ref,
    out,
    e1, x1, e2, x2, x3,
):
    top, bottom, left, right = sides(flags)
    frames, height, width, chans = feats.shape
    old = cache.shape[0]
    total = frames + old
    c2 = wc2.shape[-1]
    c3 = c2 // 2
    read = lambda ref, *ix: ref[ix].astype(F32)

    off = 8
    for f in range(total):
        for r in range(height + 4):
            if r < 2:
                own = read(up1, f, r) * top
                pa, pb, s = read(dau, f, r), read(dbu, f, r), top
            elif r < height + 2:
                own = read(cache, f, r - 2) if f < old else read(feats, f - old, r - 2)
                pa, pb, s = read(a1, f, r - 2), read(b1, f, r - 2), 1.0
            else:
                own = read(down1, f, r - height - 2) * bottom
                pa, pb, s = read(dad, f, r - height - 2), read(dbd, f, r - height - 2), bottom
            e1[f, r, off:off + width, :] = own
            e1[f, r, off - 2:off, :] = pa * (left[0] * s) + pb * (left[1] * s)
            e1[f, r, off + width:off + width + 2, :] = pa * (right[0] * s) + pb * (right[1] * s)
    gain = g1[...]
    for f in range(old, total):
        for r in range(height + 4):
            e1[f, r] = normed(e1[f, r], gain, chans)
    for k in range(3):
        for f in range(total):
            for r in range(height + 4):
                x1[k, f, r] = e1[f, r, off - 2 + k:off - 2 + k + PITCH, :].astype(BF16)
    rows1 = height + 2
    acc = None
    for t in range(3):
        for d in range(3):
            for e in range(3):
                lhs = x1[e, t:t + frames, d:d + rows1].reshape(frames * rows1 * PITCH, chans)
                term = dot_nt(lhs, w1[t, d, e])
                acc = term if acc is None else acc + term
    acc = acc.reshape(frames, rows1, PITCH, c2)

    cols = lax.broadcasted_iota(jnp.int32, (PITCH, c2), 0)
    first = 1 - flags[2]
    last = width + flags[3]
    inside = (cols >= first) & (cols <= last)
    at_top = inside & (cols < flags[0] * PITCH)
    at_bottom = inside & (cols < flags[1] * PITCH)

    gain = g2[...]
    for f in range(frames):
        for r in range(rows1):
            keep = at_top if r == 0 else at_bottom if r == rows1 - 1 else inside
            value = jnp.where(keep, acc[f, r].astype(BF16).astype(F32), 0.0)
            e2[f, r, off:off + PITCH, :] = normed(value, gain, c2)
    for k in range(3):
        for f in range(frames):
            for r in range(rows1):
                x2[k, f, r] = e2[f, r, off - 1 + k:off - 1 + k + PITCH, :].astype(BF16)

    rows2 = height + 1
    lanes = lax.broadcasted_iota(jnp.int32, (PITCH, c2), 1)
    lower = lanes < c3
    gain = g3[...]
    for q in range(2):
        parts = []
        for t in range(3):
            count = frames - (2 - t)
            acc = None
            for rs in range(2):
                for cs in range(2):
                    lhs = x2[q + cs, 0:count, rs:rs + rows2].reshape(count * rows2 * PITCH, c2)
                    term = dot_nt(lhs, wc2[((t * 2 + q) * 2 + rs) * 2 + cs])
                    acc = term if acc is None else acc + term
            parts.append(acc.reshape(count, rows2, PITCH, c2))
        for f in range(frames):
            for r in range(rows2):
                value = parts[2][f, r]
                if f >= 1:
                    value = value + parts[1][f - 1, r]
                if f >= 2:
                    value = value + parts[0][f - 2, r]
                else:
                    value = value + part2[q, f, r]
                keep = inside
                if r == 0:
                    keep = (lower & inside) | at_top
                if r == rows2 - 1:
                    keep = (~lower & inside) | at_bottom
                value = jnp.where(keep, value.astype(BF16).astype(F32), 0.0)
                square = value * value
                sum_low = jnp.sum(jnp.where(lower, square, 0.0), axis=-1, keepdims=True)
                sum_high = jnp.sum(jnp.where(lower, 0.0, square), axis=-1, keepdims=True)
                scale = jnp.where(
                    lower,
                    lax.rsqrt(sum_low * (1.0 / c3) + EPS),
                    lax.rsqrt(sum_high * (1.0 / c3) + EPS),
                )
                value = value * scale * gain
                e2[f, r, off:off + PITCH, :] = value / (1.0 + jnp.exp(-value))
        for f in range(frames):
            for r in range(rows2):
                for cs in ((1, 3) if q == 0 else (0, 2)):
                    start = off + (0, 1, 1, 2)[cs]
                    x3[cs, f, r] = e2[f, r, start:start + width, :].astype(BF16)

    acc = None
    for rs in range(2):
        for cs in range(4):
            lhs = x3[cs, :, rs:rs + height].reshape(frames * height * width, c2)
            base = (rs * 4 + cs) * 192
            term = dot_nt(lhs, wc3[base:base + 192])
            acc = term if acc is None else acc + term
    size = height * width
    acc = acc.reshape(frames, size, 192)
    turned = []
    for f in range(frames):
        value = acc[f, :, 0:64]
        if f >= 1:
            value = value + acc[f - 1, :, 64:128]
        value = value + (acc[f - 2, :, 128:192] if f >= 2 else part3[f])
        value = value.T
        turned.append(jnp.concatenate([value[b * 16:(b + 1) * 16] for b in range(4)], -1))
    turned = jnp.concatenate(turned, 0)
    result = None
    for _ in range(3):
        piece = turned.astype(BF16)
        turned = turned - piece.astype(F32)
        term = jnp.dot(piece, spread_ref[...], preferred_element_type=F32)
        result = term if result is None else result + term
    for f in range(frames):
        for c in range(out.shape[1]):
            for r in range(height):
                out[f, c, 4 * r:4 * r + 4, :] = result[
                    f * 16 + c * 4:f * 16 + c * 4 + 4, r * 4 * width:(r + 1) * 4 * width
                ]


def body(count, features, cache_first, cache_second, cache_third, w1, w2, w3, g1, g2, g3):
    tile_rows = count // TILES_X
    place = (lax.axis_index("tile") + TILES_X // 2) % count
    col, row = place % TILES_X, place // TILES_X
    odd_col, odd_row = col % 2 == 1, row % 2 == 1
    flags = jnp.stack([row > 0, row < tile_rows - 1, col > 0, col < TILES_X - 1, odd_col]).astype(jnp.int32)

    last_dims = lambda v: v[:, :, 0].transpose(0, 2, 3, 1)
    feats, old1, old2, old3 = map(last_dims, (features, cache_first, cache_second, cache_third))
    frames, height, width, _ = feats.shape
    old = old1.shape[0]
    c2, c3 = old2.shape[-1], old3.shape[-1]

    def rows_of(values, size, odd):
        return edge(values, 1, size, odd_row if odd else ~odd_row)

    def cols_of(values, size, odd):
        return edge(values, 2, size, odd_col if odd else ~odd_col)

    def third_rows(values):
        return values.reshape(old, 2, -1, c3)

    def third_cols(values):
        return values.reshape(old, -1, 2, c3)

    def third_corner(values):
        return jnp.broadcast_to(values, (old, 2, 2, c3))

    row_pairs = [0] if tile_rows <= 2 else [0, 1]
    first = lambda f: jnp.concatenate([f(old1), f(feats)], 0)
    rows2, rows1, corners = {}, {}, {}
    for rp in row_pairs:
        rows2[rp] = swap(joined(rows_of(old2, 2, rp), third_rows(rows_of(old3, 1, rp))), count, rp, None)
    sent = {}
    for cp in (0, 1):
        x1 = first(lambda v: cols_of(v, 2, cp))
        x2 = joined(cols_of(old2, 2, cp), third_cols(cols_of(old3, 1, cp)))
        x1 = x1.reshape(-1, 2, x1.shape[-1])
        x2 = x2.reshape(-1, 2, x2.shape[-1])
        sent[cp] = swap(jnp.concatenate([x1, x2], 0), count, None, cp)
        for rp in row_pairs:
            y1 = first(lambda v: cols_of(rows_of(v, 2, rp), 2, cp))
            y2 = joined(
                cols_of(rows_of(old2, 2, rp), 2, cp),
                third_corner(cols_of(rows_of(old3, 1, rp), 1, cp)),
            )
            y1 = y1.reshape(-1, 2, y1.shape[-1])
            y2 = y2.reshape(-1, 2, y2.shape[-1])
            corners[rp, cp] = swap(jnp.concatenate([y1, y2], 0), count, rp, cp)
    for rp in row_pairs:
        rows1[rp] = swap(first(lambda v: rows_of(v, 2, rp)), count, rp, None)

    def above(pieces):
        return pieces[0] if len(pieces) == 1 else jnp.where(odd_row, pieces[0], pieces[1])

    def below(pieces):
        return pieces[0] if len(pieces) == 1 else jnp.where(odd_row, pieces[1], pieces[0])

    up1, down1 = above(rows1), below(rows1)
    up2, down2 = above(rows2), below(rows2)
    cut_side = (frames + old) * height
    cut_corner = (frames + old) * 2
    side1 = [sent[cp][:cut_side].reshape(frames + old, height, 2, -1) for cp in (0, 1)]
    side2 = [sent[cp][cut_side:].reshape(old, 2 * height, 2, -1) for cp in (0, 1)]
    diagonals = [
        pick({rp: corners[rp, cp] for rp in row_pairs}) for pick in (above, below) for cp in (0, 1)
    ]
    corner1 = [v[:cut_corner].reshape(frames + old, 2, 2, -1) for v in diagonals]
    corner2 = [v[cut_corner:].reshape(old, 2, 2, -1) for v in diagonals]

    rgb = w3.shape[3]
    flat3 = w3.reshape(27 * rgb, c3)
    flat3 = jnp.pad(flat3, ((0, 96 - 27 * rgb), (0, 0)))
    w3_all = jnp.concatenate(
        [
            jnp.pad(flat3, ((0, 0), (0, 192 - c3))),
            jnp.pad(flat3, ((0, 0), (0, 192 - c3))),
            jnp.pad(flat3, ((0, 0), (c3, 192 - 2 * c3))),
        ],
        0,
    )

    smem = pl.BlockSpec(memory_space=pltpu.SMEM)
    vmem = pl.BlockSpec(memory_space=pltpu.VMEM)
    size = height * width
    part2, part3, wc2, wc3 = pl.pallas_call(
        history_kernel,
        out_shape=[
            jax.ShapeDtypeStruct((2, 2, height + 1, PITCH, c2), F32),
            jax.ShapeDtypeStruct((2, size, 64), F32),
            jax.ShapeDtypeStruct((24, 2 * c3, c2), BF16),
            jax.ShapeDtypeStruct((8 * 192, 192), BF16),
        ],
        in_specs=[smem] + [vmem] * 14,
        out_specs=[vmem] * 4,
        scratch_shapes=[
            pltpu.VMEM((old, 2 * height + 4, 64, 128), F32),
            pltpu.VMEM((old, 2 * height + 4, 64, 128), F32),
            pltpu.VMEM((old, 4 * height + 2, 96, 128), F32),
            pltpu.VMEM((4, old, 2 * height + 4, PITCH, c2), BF16),
            pltpu.VMEM((6, old, height + 1, 4, width, 128), BF16),
            pltpu.VMEM((36 * 128, 128), BF16),
        ],
        compiler_params=pltpu.CompilerParams(vmem_limit_bytes=60 << 20),
        cost_estimate=pl.CostEstimate(flops=4_000_000_000, bytes_accessed=4_000_000, transcendentals=0),
        name="history",
    )(
        flags, old2, old3, up2, down2, *side2, *corner2, w2, w3_all,
        jnp.asarray(fine_taps(rgb), BF16), jnp.asarray(cache_taps(rgb), BF16),
    )

    out = pl.pallas_call(
        frames_kernel,
        out_shape=jax.ShapeDtypeStruct((frames, rgb, 4 * height, 4 * width), F32),
        in_specs=[smem] + [vmem] * 19,
        out_specs=vmem,
        scratch_shapes=[
            pltpu.VMEM((frames + old, height + 4, 40, feats.shape[-1]), F32),
            pltpu.VMEM((3, frames + old, height + 4, PITCH, feats.shape[-1]), BF16),
            pltpu.VMEM((frames, height + 2, 40, c2), F32),
            pltpu.VMEM((3, frames, height + 2, PITCH, c2), BF16),
            pltpu.VMEM((4, frames, height + 1, width, c2), BF16),
        ],
        compiler_params=pltpu.CompilerParams(vmem_limit_bytes=60 << 20),
        cost_estimate=pl.CostEstimate(flops=10_000_000_000, bytes_accessed=8_000_000, transcendentals=0),
        name="frames",
    )(
        flags, feats, old1, up1, down1, *side1, *corner1, w1, g1[None], g2[None],
        jnp.concatenate([g3, g3])[None], part2, part3, wc2, wc3,
        jnp.asarray(spread(height, width), BF16),
    )
    return out[:, :, None]


def solution(mesh):
    tiled = P("groups", None, "tile", None, None)
    return jax.shard_map(
        functools.partial(body, mesh.shape["tile"]),
        mesh=mesh,
        in_specs=(tiled,) * 4 + (P(),) * 6,
        out_specs=tiled,
        check_vma=False,
    )
```

profile of v0, /device:TPU:0, one launch (start us, length us, event | category | flops | bytes accessed | tf_op | source)
XLA Modules:
  0.0 63.0 jit_solution(5146264072432627795)
XLA Ops:
  0.0 0.0 copy-start
  0.0 0.1 pad.38.clone
  0.1 0.1 pad.36.clone
  0.2 0.8 %slice_select_fusion.3 = bf16[2,1,64,96]{3,2,1,0:T(8,128)(2,1)S(1)} fusion(bf16[2,32,64,96]{3,2,1,0:T(8,128)(2,1)} %bitcast.73, pred[]{:T(512)S(6)} %not.4), kind=kLoop, calls=%fused_computation.20 | loop fusion | flops 12288 | bytes 73729 | tf_op jit(solution)/shard_map/jit(_where)/select_n | solution.py:45
  1.0 0.8 %slice_select_fusion.2 = bf16[2,2,16,384]{3,2,1,0:T(8,128)(2,1)S(1)} fusion(bf16[2,8,16,384]{3,2,1,0:T(8,128)(2,1)} %bitcast.53, pred[]{:T(512)S(6)} %not.4), kind=kLoop, calls=%fused_computation.17 | loop fusion | flops 24576 | bytes 147457 | tf_op jit(solution)/shard_map/jit(_where)/select_n | solution.py:45
  1.8 0.9 %slice_select_fusion.1 = bf16[2,2,32,192]{3,2,1,0:T(8,128)(2,1)S(1)} fusion(bf16[2,16,32,192]{3,2,1,0:T(8,128)(2,1)} %bitcast.56, pred[]{:T(512)S(6)} %not.4), kind=kLoop, calls=%fused_computation.12 | loop fusion | flops 24576 | bytes 147457 | tf_op jit(solution)/shard_map/jit(_where)/select_n | solution.py:45
  2.7 1.0 %slice_select_fusion = bf16[4,2,16,384]{3,2,1,0:T(8,128)(2,1)S(1)} fusion(bf16[4,8,16,384]{3,2,1,0:T(8,128)(2,1)} %bitcast.47, pred[]{:T(512)S(6)} %not.4), kind=kLoop, calls=%fused_computation.6 | loop fusion | flops 49152 | bytes 294913 | tf_op jit(solution)/shard_map/jit(_where)/select_n | solution.py:45
  3.8 0.1 pad_maximum_fusion.5
  3.9 5.4 %collective-permute-start.4 = (bf16[16,2,384]{2,1,0:T(2,128)(2,1)S(1)}, bf16[16,2,384]{2,1,0:T(2,128)(2,1)S(1)}, u32[]{:S(2)}, u32[]{:S(2)}) collective-permute-start(bf16[16,2,384]{2,1,0:T(2,128)(2,1)S(1)} %pad_maximum_fusion.4), channel_id=1, source_target_pairs={{0,7},{1,10},{2,9},{3,3},{4,4},{5,14},{6,13},{7,0},{8,15},{9,2},{1... | collective-permute-start | bytes 73736 | tf_op jit(solution)/shard_map/ppermute | solution.py:38
  9.4 1.7 %collective-permute-start.3 = (bf16[16,2,384]{2,1,0:T(2,128)(2,1)S(1)}, bf16[16,2,384]{2,1,0:T(2,128)(2,1)S(1)}, u32[]{:S(2)}, u32[]{:S(2)}) collective-permute-start(bf16[16,2,384]{2,1,0:T(2,128)(2,1)S(1)} %pad_maximum_fusion.3), channel_id=1, source_target_pairs={{0,9},{1,8},{2,11},{3,10},{4,13},{5,12},{6,15},{7,14},{8,1},{9,0},... | collective-permute-start | bytes 73736 | tf_op jit(solution)/shard_map/ppermute | solution.py:38
  11.2 2.7 %collective-permute-start.5 = (bf16[2,2,32,384]{3,2,1,0:T(8,128)(2,1)S(1)}, bf16[2,2,32,384]{3,2,1,0:T(8,128)(2,1)S(1)}, u32[]{:S(2)}, u32[]{:S(2)}) collective-permute-start(bf16[2,2,32,384]{3,2,1,0:T(8,128)(2,1)S(1)} %maximum_maximum_fusion.2), channel_id=1, source_target_pairs={{0,8},{1,9},{2,10},{3,11},{4,12},{5,13},{6,14},{7,15},{8,0},{9,1},... | collective-permute-start | bytes 294920 | tf_op jit(solution)/shard_map/ppermute | solution.py:38
  13.8 1.0 %broadcast_select_fusion.6 = (bf16[2,8,2,384]{3,2,1,0:T(2,128)(2,1)S(1)}, bf16[2,8,2,384]{3,2,1,0:T(2,128)(2,1)S(1)}) fusion(pred[]{:T(512)} %eq.11, bf16[2,8,16,384]{3,2,1,0:T(8,128)(2,1)} %bitcast.54, pred[]{:T(512)S(6)} %not.5), kind=kLoop, calls=%fused_computation.18 | loop fusion | flops 24576 | bytes 98306 | tf_op jit(solution)/shard_map/jit(_where)/select_n | solution.py:45
  14.8 1.1 %broadcast_select_fusion.3 = (bf16[2,16,2,192]{3,2,1,0:T(2,128)(2,1)S(1)}, bf16[2,16,2,192]{3,2,1,0:T(2,128)(2,1)S(1)}) fusion(pred[]{:T(512)} %eq.11, bf16[2,16,32,192]{3,2,1,0:T(8,128)(2,1)} %bitcast.57, pred[]{:T(512)S(6)} %not.5), kind=kLoop, calls=%fused_computation.14 | loop fusion | flops 24576 | bytes 98306 | tf_op jit(solution)/shard_map/jit(_where)/select_n | solution.py:45
  15.9 1.1 %broadcast_select_fusion.2 = (bf16[2,32,1,96]{3,2,1,0:T(2,128)(2,1)S(1)}, bf16[2,32,1,96]{3,2,1,0:T(2,128)(2,1)S(1)}) fusion(pred[]{:T(512)} %eq.11, bf16[2,32,64,96]{3,2,1,0:T(8,128)(2,1)} %bitcast.74, pred[]{:T(512)S(6)} %not.5), kind=kLoop, calls=%fused_computation.13 | loop fusion | flops 12288 | bytes 49154 | tf_op jit(solution)/shard_map/jit(_where)/select_n | solution.py:45
  16.9 1.1 %broadcast_select_fusion = (bf16[4,8,2,384]{3,2,1,0:T(2,128)(2,1)S(1)}, bf16[4,8,2,384]{3,2,1,0:T(2,128)(2,1)S(1)}) fusion(pred[]{:T(512)} %eq.11, bf16[4,8,16,384]{3,2,1,0:T(8,128)(2,1)} %bitcast.48, pred[]{:T(512)S(6)} %not.5), kind=kLoop, calls=%fused_computation.8 | loop fusion | flops 49152 | bytes 196610 | tf_op jit(solution)/shard_map/jit(_where)/select_n | solution.py:45
  18.1 0.1 pad.50.clone
  18.2 0.1 pad.52.clone
  18.3 0.2 pad_maximum_fusion.1
  18.5 0.4 maximum_maximum_fusion.1
  18.9 2.7 %collective-permute-start.2 = (bf16[80,2,384]{2,1,0:T(2,128)(2,1)S(1)}, bf16[80,2,384]{2,1,0:T(2,128)(2,1)S(1)}, u32[]{:S(2)}, u32[]{:S(2)}) collective-permute-start(bf16[80,2,384]{2,1,0:T(2,128)(2,1)S(1)} %get-tuple-element.21), channel_id=1, source_target_pairs={{0,15},{1,2},{2,1},{3,3},{4,4},{5,6},{6,5},{7,8},{8,7},{9,10},{10,... | collective-permute-start | bytes 368648 | tf_op jit(solution)/shard_map/ppermute | solution.py:38
  21.5 0.1 collective-permute-start.1
  21.6 0.0 copy-done
  21.7 0.7 %fusion.1.w3 = bf16[288,192]{1,0:T(8,128)(2,1)} fusion(bf16[96,96]{1,0:T(8,128)(2,1)S(1)} %pad.13, bf16[96,192]{1,0:T(8,128)(2,1)S(1)} %pad.14), kind=kLoop, calls=%fused_computation.2 | loop fusion | flops 442368 | bytes 165888 | tf_op jit(solution)/shard_map/concatenate | solution.py:462
  22.4 0.0 copy-done.4
  22.4 0.7 %pad_maximum_fusion.7 = f32[192]{0:T(256)} fusion(f32[96]{0:T(128)S(1)} %copy-done.4), kind=kLoop, calls=%fused_computation.35 | loop fusion | flops 192 | bytes 1152 | tf_op jit(solution)/shard_map/concatenate | solution.py:517
  23.1 0.1 stack.23
  23.2 0.5 convert_element_type.10.flags
  23.7 0.0 copy-done.1
  23.7 0.5 broadcast_in_dim.36.g1
  24.3 0.0 collective-permute-done.4
  24.3 1.4 %collective-permute-start = (bf16[6,2,16,384]{3,2,1,0:T(8,128)(2,1)S(1)}, bf16[6,2,16,384]{3,2,1,0:T(8,128)(2,1)S(1)}, u32[]{:S(2)}, u32[]{:S(2)}) collective-permute-start(bf16[6,2,16,384]{3,2,1,0:T(8,128)(2,1)S(1)} %pad_maximum_fusion), channel_id=1, source_target_pairs={{0,8},{1,9},{2,10},{3,11},{4,12},{5,13},{6,14},{7,15},{8,0},{9,1},... | collective-permute-start | bytes 442376 | tf_op jit(solution)/shard_map/ppermute | solution.py:38
  25.7 0.6 slice.195
  26.3 0.6 slice.191
  26.9 0.0 collective-permute-done.3
  26.9 0.6 slice.194
  27.5 0.6 slice.190
  28.1 0.0 collective-permute-done.2
  28.1 0.7 %slice.193 = bf16[32,2,384]{2,1,0:T(2,128)(2,1)} slice(bf16[80,2,384]{2,1,0:T(2,128)(2,1)S(1)} %collective-permute-done.2), slice={[48:80], [0:2], [0:384]} | slice | bytes 98304 | tf_op jit(solution)/shard_map/slice | solution.py:452
  28.8 0.0 collective-permute-done.1
  28.8 0.6 %slice.192 = bf16[32,2,384]{2,1,0:T(2,128)(2,1)} slice(bf16[80,2,384]{2,1,0:T(2,128)(2,1)S(1)} %collective-permute-done.1), slice={[48:80], [0:2], [0:384]} | slice | bytes 98304 | tf_op jit(solution)/shard_map/slice | solution.py:452
  29.4 0.0 collective-permute-done.5.up2.down2
  29.4 0.6 %copy-done.3 = bf16[2,2,32,384]{3,2,1,0:T(8,128)(2,1)} copy-done((bf16[2,2,32,384]{3,2,1,0:T(8,128)(2,1)}, bf16[2,2,32,384]{3,2,1,0:T(8,128)(2,1)S(1)}, u32[]{:S(2)}) %copy-start.3) | copy-done | bytes 98328
  30.0 8.4 %history.1 = (f32[2,2,9,24,192]{4,3,2,1,0:T(8,128)}, f32[2,128,64]{2,1,0:T(8,128)}, bf16[24,192,192]{2,1,0:T(8,128)(2,1)}, bf16[1536,192]{1,0:T(8,128)(2,1)}) custom-call(s32[5]{0:T(128)} %convert_element_type.10.flags, bf16[2,16,32,192]{3,2,1,0:T(8,128)(2,1)} %bitcast.58, bf16[2,32,64,96]{3,2,1,0:T(8,128)(2,1)} %bitcast.75, ...), custom_call_target="tpu_custom_call" | custom-call | flops 4000000000 | bytes 4000000 | tf_op jit(solution)/shard_map/history/pallas_call | solution.py:474
  38.4 0.7 %slice.177 = bf16[48,2,384]{2,1,0:T(2,128)(2,1)} slice(bf16[80,2,384]{2,1,0:T(2,128)(2,1)S(1)} %collective-permute-done.2), slice={[0:48], [0:2], [0:384]} | slice | bytes 147456 | tf_op jit(solution)/shard_map/slice | solution.py:451
  39.1 0.7 %slice.176 = bf16[48,2,384]{2,1,0:T(2,128)(2,1)} slice(bf16[80,2,384]{2,1,0:T(2,128)(2,1)S(1)} %collective-permute-done.1), slice={[0:48], [0:2], [0:384]} | slice | bytes 147456 | tf_op jit(solution)/shard_map/slice | solution.py:451
  39.8 0.0 collective-permute-done.up1.down1
  39.8 0.7 %copy-done.2 = bf16[6,2,16,384]{3,2,1,0:T(8,128)(2,1)} copy-done((bf16[6,2,16,384]{3,2,1,0:T(8,128)(2,1)}, bf16[6,2,16,384]{3,2,1,0:T(8,128)(2,1)S(1)}, u32[]{:S(2)}) %copy-start.2) | copy-done | bytes 147480
  40.5 22.5 %frames.1 = f32[4,3,32,64]{3,2,1,0:T(8,128)} custom-call(s32[5]{0:T(128)} %convert_element_type.10.flags, bf16[4,8,16,384]{3,2,1,0:T(8,128)(2,1)} %bitcast.49, bf16[2,8,16,384]{3,2,1,0:T(8,128)(2,1)} %bitcast.55, bf16[6,2,16,384]{3,2,1,0:T(8,128)(2,1)} %copy-done.2, bf16[6,2,16,384]{3,2,1,0:T(8,128)(2,1)} %copy-done.2, bf16[6,8,2,384]{3,2,1,0:T(2,128)(2,1)} %bitcast.60, ...), custom_call_target="tpu_custom_call" | custom-call | flops 10000000000 | bytes 8000000 | tf_op jit(solution)/shard_map/frames/pallas_call | solution.py:500
  (25 shorter events, 0.3 us)
Async XLA Ops:
  0.0 21.6 %copy-start = (bf16[3,3,3,3,96]{4,3,2,1,0:T(4,128)(2,1)S(1)}, bf16[3,3,3,3,96]{4,3,2,1,0:T(4,128)(2,1)}, u32[]{:S(2)}) copy-start(bf16[3,3,3,3,96]{4,3,2,1,0:T(4,128)(2,1)} %param.19) | copy-start | bytes 46660
  0.0 22.4 %copy-start.4 = (f32[96]{0:T(128)S(1)}, f32[96]{0:T(128)}, u32[]{:S(2)}) copy-start(f32[96]{0:T(128)} %param.22) | copy-start | bytes 1156
  0.0 23.7 %copy-start.1 = (f32[384]{0:T(512)S(1)}, f32[384]{0:T(512)}, u32[]{:S(2)}) copy-start(f32[384]{0:T(512)} %param.20) | copy-start | bytes 4612
  3.9 20.4 %collective-permute-start.4 = (bf16[16,2,384]{2,1,0:T(2,128)(2,1)S(1)}, bf16[16,2,384]{2,1,0:T(2,128)(2,1)S(1)}, u32[]{:S(2)}, u32[]{:S(2)}) collective-permute-start(bf16[16,2,384]{2,1,0:T(2,128)(2,1)S(1)} %pad_maximum_fusion.4), channel_id=1, source_target_pairs={{0,7},{1,10},{2,9},{3,3},{4,4},{5,14},{6,13},{7,0},{8,15},{9,2},{1... | collective-permute-start | bytes 73736 | tf_op jit(solution)/shard_map/ppermute | solution.py:38
  9.4 17.5 %collective-permute-start.3 = (bf16[16,2,384]{2,1,0:T(2,128)(2,1)S(1)}, bf16[16,2,384]{2,1,0:T(2,128)(2,1)S(1)}, u32[]{:S(2)}, u32[]{:S(2)}) collective-permute-start(bf16[16,2,384]{2,1,0:T(2,128)(2,1)S(1)} %pad_maximum_fusion.3), channel_id=1, source_target_pairs={{0,9},{1,8},{2,11},{3,10},{4,13},{5,12},{6,15},{7,14},{8,1},{9,0},... | collective-permute-start | bytes 73736 | tf_op jit(solution)/shard_map/ppermute | solution.py:38
  11.2 18.3 %collective-permute-start.5 = (bf16[2,2,32,384]{3,2,1,0:T(8,128)(2,1)S(1)}, bf16[2,2,32,384]{3,2,1,0:T(8,128)(2,1)S(1)}, u32[]{:S(2)}, u32[]{:S(2)}) collective-permute-start(bf16[2,2,32,384]{3,2,1,0:T(8,128)(2,1)S(1)} %maximum_maximum_fusion.2), channel_id=1, source_target_pairs={{0,8},{1,9},{2,10},{3,11},{4,12},{5,13},{6,14},{7,15},{8,0},{9,1},... | collective-permute-start | bytes 294920 | tf_op jit(solution)/shard_map/ppermute | solution.py:38
  18.9 9.2 %collective-permute-start.2 = (bf16[80,2,384]{2,1,0:T(2,128)(2,1)S(1)}, bf16[80,2,384]{2,1,0:T(2,128)(2,1)S(1)}, u32[]{:S(2)}, u32[]{:S(2)}) collective-permute-start(bf16[80,2,384]{2,1,0:T(2,128)(2,1)S(1)} %get-tuple-element.21), channel_id=1, source_target_pairs={{0,15},{1,2},{2,1},{3,3},{4,4},{5,6},{6,5},{7,8},{8,7},{9,10},{10,... | collective-permute-start | bytes 368648 | tf_op jit(solution)/shard_map/ppermute | solution.py:38
  21.5 7.2 %collective-permute-start.1 = (bf16[80,2,384]{2,1,0:T(2,128)(2,1)S(1)}, bf16[80,2,384]{2,1,0:T(2,128)(2,1)S(1)}, u32[]{:S(2)}, u32[]{:S(2)}) collective-permute-start(bf16[80,2,384]{2,1,0:T(2,128)(2,1)S(1)} %get-tuple-element.22), channel_id=1, source_target_pairs={{0,1},{1,0},{2,3},{3,2},{4,5},{5,4},{6,7},{7,6},{8,9},{9,8},{10,11... | collective-permute-start | bytes 368648 | tf_op jit(solution)/shard_map/ppermute | solution.py:38
  24.3 15.5 %collective-permute-start = (bf16[6,2,16,384]{3,2,1,0:T(8,128)(2,1)S(1)}, bf16[6,2,16,384]{3,2,1,0:T(8,128)(2,1)S(1)}, u32[]{:S(2)}, u32[]{:S(2)}) collective-permute-start(bf16[6,2,16,384]{3,2,1,0:T(8,128)(2,1)S(1)} %pad_maximum_fusion), channel_id=1, source_target_pairs={{0,8},{1,9},{2,10},{3,11},{4,12},{5,13},{6,14},{7,15},{8,0},{9,1},... | collective-permute-start | bytes 442376 | tf_op jit(solution)/shard_map/ppermute | solution.py:38
  29.4 0.6 %copy-start.3 = (bf16[2,2,32,384]{3,2,1,0:T(8,128)(2,1)}, bf16[2,2,32,384]{3,2,1,0:T(8,128)(2,1)S(1)}, u32[]{:S(2)}) copy-start(bf16[2,2,32,384]{3,2,1,0:T(8,128)(2,1)S(1)} %collective-permute-done.5.up2.down2) | copy-start | bytes 294916
  39.8 0.7 %copy-start.2 = (bf16[6,2,16,384]{3,2,1,0:T(8,128)(2,1)}, bf16[6,2,16,384]{3,2,1,0:T(8,128)(2,1)S(1)}, u32[]{:S(2)}) copy-start(bf16[6,2,16,384]{3,2,1,0:T(8,128)(2,1)S(1)} %collective-permute-done.up1.down1) | copy-start | bytes 442372
where the time goes:
time: 63.4 us; the launch traced here: 63 us
  Pallas kernels  30.9 us (49%)
  starting transfers between devices  13.9 us (22%)
  other arithmetic  10.5 us (17%)
  local copies, waits for them, and re-layouts  7.44 us (12%)
    pallas_call x1, Pallas kernels, body(): pl.pallas_call(frames_kernel, out_shape=jax.ShapeDtypeStruct((frames, rgb...  22.5 us
    ppermute x6, starting transfers between devices, swap(): return lax.ppermute(values, 'tile', pairs_of(count, row_pair, col_pair))  13.9 us
    pallas_call x1, Pallas kernels, body(): pl.pallas_call(history_kernel, out_shape=[jax.ShapeDtypeStruct((2, 2, hei...  8.4 us
    select_n x12, other arithmetic, edge(): return jnp.where(last, tail, head)  7.79 us
    slice x2, local copies, waits for them, and re-layouts, body(): sent[cp][:cut_side].reshape(frames + old, height, 2, -1)  1.37 us
    unnamed x13, local copies, waits for them, and re-layouts  1.32 us
    slice x2, local copies, waits for them, and re-layouts, body(): sent[cp][cut_side:].reshape(old, 2 * height, 2, -1)  1.3 us
  transfers between devices with their start and end apart: 6, of which 0 were waited for; matrix products, arithmetic and copies ran while one was open for 20% of the time, Pallas kernels for 13%

commit v1 on v0

v1 whole, which is shorter than its diff:
```python
import functools

import jax
import jax.numpy as jnp
import numpy as np
from jax import lax
from jax.experimental import pallas as pl
from jax.experimental.pallas import tpu as pltpu
from jax.sharding import PartitionSpec as P


TILES_X = 8
EPS = 1e-06
F32 = jnp.float32
BF16 = jnp.bfloat16
PITCH = 24


def partner(index, size, odd):
    other = index ^ 1 if not odd else ((index - 1) ^ 1) + 1
    return other if 0 <= other < size and (not odd or index > 0) else index


def pairs_of(count, row_pair, col_pair):
    rows = count // TILES_X
    out = []
    for k in range(count):
        m = (k + TILES_X // 2) % count
        r, c = divmod(m, TILES_X)
        r2 = r if row_pair is None else partner(r, rows, row_pair)
        c2 = c if col_pair is None else partner(c, TILES_X, col_pair)
        if (row_pair is not None and r2 == r) or (col_pair is not None and c2 == c):
            r2, c2 = r, c
        out.append((k, (r2 * TILES_X + c2 - TILES_X // 2) % count))
    return out


def swap(values, count, row_pair, col_pair):
    return lax.ppermute(values, "tile", pairs_of(count, row_pair, col_pair))


@functools.lru_cache
def fine_taps(rgb):
    slots = np.zeros((2, 4, 3, 4, 4, 4, 2, 3, 3, 3, rgb), np.float32)
    for a in range(4):
        for d in range(3):
            row = (a + d - 1) // 2
            rs, half = {-1: (0, 1), 0: (0, 0), 1: (1, 1), 2: (1, 0)}[row]
            for b in range(4):
                for e in range(3):
                    cs = (b + e - 1) // 2 + 1
                    for t in range(3):
                        for c in range(rgb):
                            slots[rs, cs, 2 - t, b, c, a, half, t, d, e, c] += 1
    flat = slots.reshape(8 * 192, 2, 27 * rgb)
    return np.pad(flat, ((0, 0), (0, 0), (0, 96 - 27 * rgb))).reshape(8 * 192, 192)


@functools.lru_cache
def cache_taps(rgb):
    slots = np.zeros((6, 6, 2, 4, 4, 4, 3, 3, 3, rgb), np.float32)
    for a in range(4):
        for d in range(3):
            for b in range(4):
                for e in range(3):
                    for t in range(2):
                        for c in range(rgb):
                            slots[a + d, b + e, 1 - t, b, c, a, t, d, e, c] += 1
    flat = slots.reshape(36 * 128, 27 * rgb)
    return np.pad(flat, ((0, 0), (0, 96 - 27 * rgb)))


@functools.lru_cache
def spread(height, width):
    out = np.zeros((4, height, width, height, width, 4), np.float32)
    for b in range(4):
        for r in range(height):
            for c in range(width):
                out[b, r, c, r, c, b] = 1
    return out.reshape(4 * height * width, 4 * height * width)


def dot_nt(lhs, rhs):
    return lax.dot_general(lhs, rhs, (((1,), (1,)), ((), ())), preferred_element_type=F32)


def position(count):
    place = lax.rem(lax.axis_index("tile") + TILES_X // 2, count)
    col, row = lax.rem(place, TILES_X), lax.div(place, TILES_X)
    flag = lambda v: v.astype(jnp.int32)
    return (
        flag(row > 0), flag(row < count // TILES_X - 1), flag(col > 0), flag(col < TILES_X - 1),
        lax.rem(col, 2), lax.rem(row, 2),
    )


def sides(flags):
    top, bottom, left, right, odd = flags[:5]
    as_f = lambda v: v.astype(F32)
    return (
        as_f(top),
        as_f(bottom),
        (as_f(left * odd), as_f(left * (1 - odd))),
        (as_f(right * (1 - odd)), as_f(right * odd)),
    )


def pack_kernel(count, row_pairs, feats_hbm, old1_hbm, old2_hbm, old3_hbm, *refs):
    *outs, feats, old1, old2, old3, near3, far3, sems = refs
    wide3 = old3_hbm.shape[2]
    copies = [
        pltpu.make_async_copy(src, dst, sems.at[i])
        for i, (src, dst) in enumerate((
            (feats_hbm, feats), (old1_hbm, old1), (old2_hbm, old2),
            (old3_hbm.at[:, pl.ds(0, 1)], old3.at[:, pl.ds(0, 1)]),
            (old3_hbm.at[:, pl.ds(old3_hbm.shape[1] - 1, 1)], old3.at[:, pl.ds(1, 1)]),
            (old3_hbm.at[:, :, pl.ds(0, 8)], near3),
            (old3_hbm.at[:, :, pl.ds(wide3 - 8, 8)], far3),
        ))
    ]
    for copy in copies:
        copy.start()
    *_, odd_col, odd_row = position(count)
    for copy in copies:
        copy.wait()
    firsts = [old1.at[f] for f in range(old1.shape[0])] + [feats.at[f] for f in range(feats.shape[0])]
    _, height, width, _ = feats.shape
    c2, c3 = old2.shape[-1], old3.shape[-1]
    aside = slice(256, 256 + c3)
    total = len(firsts)
    outs = list(outs)
    sides_out = {0: outs.pop(0), 1: outs.pop(0)}
    for rp in row_pairs:
        rows2, rows1 = outs.pop(0), outs.pop(0)
        low = odd_row if rp else 1 - odd_row
        start1, start2, start3 = low * (height - 2), low * (2 * height - 2), low
        for i, ref in enumerate(firsts):
            rows1[i] = ref[pl.ds(start1, 2)]
        half = 2 * width
        for f in range(old2.shape[0]):
            rows2[f, :, :, 0:c2] = old2[f, pl.ds(start2, 2)]
            for j in range(2):
                rows2[f, j, :, aside] = old3[f, start3, j * half:(j + 1) * half, :]
        for cp in (0, 1):
            corner = outs.pop(0)
            far = odd_col if cp else 1 - odd_col
            for value in (0, 1):
                @pl.when(far == value)
                def _():
                    pick = lambda n, size: slice(value * (n - size), value * (n - size) + size)
                    for i, ref in enumerate(firsts):
                        corner[2 * i:2 * i + 2] = ref[pl.ds(start1, 2), pick(width, 2), :]
                    for f in range(old2.shape[0]):
                        at = 2 * total + 2 * f
                        corner[at:at + 2, :, 0:c2] = old2[f, pl.ds(start2, 2), pick(2 * width, 2), :]
                        corner[at, 0:1, aside] = old3[f, start3, pick(wide3, 1), :]
    for cp in (0, 1):
        side = sides_out[cp]
        far = odd_col if cp else 1 - odd_col
        for value in (0, 1):
            @pl.when(far == value)
            def _():
                pick = lambda n, size: slice(value * (n - size), value * (n - size) + size)
                for i, ref in enumerate(firsts):
                    side[height * i:height * (i + 1)] = ref[:, pick(width, 2), :]
                for f in range(old2.shape[0]):
                    at = height * total + 2 * height * f
                    side[at:at + 2 * height, :, 0:c2] = old2[f, :, pick(2 * width, 2), :]
                    for r in range(2 * height):
                        ends = near3 if value == 0 else far3
                        pair = [ends[f, 2 * r + j, pick(8, 1), :].astype(F32) for j in range(2)]
                        side[at + r, :, aside] = jnp.concatenate(pair, 0).astype(BF16)


def weights_kernel(w2, w3, taps3, taps3c, wc2, wc3, w3c, flat):
    c3 = w2.shape[3]
    rgb = w3.shape[3]
    flat[...] = jnp.zeros_like(flat)
    for t in range(3):
        for d in range(3):
            for e in range(3):
                row = ((t * 3 + d) * 3 + e) * rgb
                value = w3[t, d, e].astype(F32)
                flat[row:row + rgb, 0:c3] = value
                flat[96 + row:96 + row + rgb, c3:2 * c3] = value
    three = flat[0:96, 0:128].astype(BF16)
    w3c[...] = jnp.dot(taps3c[...], three, preferred_element_type=F32).astype(BF16)
    wc3[:, 0:2 * c3] = jnp.dot(taps3[...], flat[...].astype(BF16), preferred_element_type=F32).astype(BF16)
    for t in range(3):
        rows = {}
        for e in range(3):
            w = [w2[t, d, e].astype(F32) for d in range(3)]
            rows[e] = (w[0], w[0] + w[1], w[1] + w[2], w[2])
        for q in range(2):
            for cs in range(2):
                cols = [
                    rows[0][v] if (q, cs) == (0, 0) else rows[2][v] if (q, cs) == (1, 1)
                    else rows[1][v] + (rows[2][v] if q == 0 else rows[0][v])
                    for v in range(4)
                ]
                for rs in range(2):
                    base = ((t * 2 + q) * 2 + rs) * 2 + cs
                    wc2[base, 0:c3, 0:2 * c3] = cols[2 * rs].astype(BF16)
                    wc2[base, c3:2 * c3, 0:2 * c3] = cols[2 * rs + 1].astype(BF16)
    lanes = wc2.shape[-1]
    wc2[:, :, 2 * c3:lanes] = jnp.zeros(wc2.shape[:2] + (lanes - 2 * c3,), BF16)
    wc3[:, 2 * c3:lanes] = jnp.zeros((wc3.shape[0], lanes - 2 * c3), BF16)


def history_kernel(
    count, second, third, up2, down2, side_a, side_b, dau, dbu, dad, dbd, w2, w3c,
    part2, part3,
    e_lo, e_hi, e3, xc2, xc3,
):
    top, bottom, left, right = sides(position(count))
    frames, tall, wide, chans = second.shape
    c3 = third.shape[-1]
    lo = 128
    hi = chans - lo
    read = lambda ref, *ix: ref[ix].astype(F32)
    skip = side_a.shape[0] - frames * tall
    skip_corner = dau.shape[0] - frames * 2
    at_side = lambda ref, f, r: read(ref, skip + f * tall + r)
    at_corner = lambda ref, f, r: read(ref, skip_corner + 2 * f + r)

    off = 8

    def put2(f, row, col, value):
        n = value.shape[0]
        e_lo[f, row, col:col + n, :] = value[:, :lo]
        e_hi[f, row, col:col + n, 0:hi] = value[:, lo:chans]

    for f in range(frames):
        for r in range(tall + 4):
            if r < 2:
                own = read(up2, f, r) * top
                pa, pb, s = at_corner(dau, f, r), at_corner(dbu, f, r), top
            elif r < tall + 2:
                own = read(second, f, r - 2)
                pa, pb, s = at_side(side_a, f, r - 2), at_side(side_b, f, r - 2), 1.0
            else:
                own = read(down2, f, r - tall - 2) * bottom
                pa, pb, s = at_corner(dad, f, r - tall - 2), at_corner(dbd, f, r - tall - 2), bottom
            put2(f, r, off, own)
            put2(f, r, off - 2, pa * (left[0] * s) + pb * (left[1] * s))
            put2(f, r, off + wide, pa * (right[0] * s) + pb * (right[1] * s))
    for k in range(4):
        for f in range(frames):
            for r in range(tall + 4):
                cols = pl.ds(off - 3 + k, PITCH, stride=2)
                xc2[k, f, r, :, 0:lo] = e_lo[f, r, cols, :].astype(BF16)
                xc2[k, f, r, :, lo:chans] = e_hi[f, r, cols, :].astype(BF16)[:, :hi]
    rows_out = tall + 2
    for q in range(2):
        acc = None
        for d in range(3):
            for e in range(3):
                lhs = xc2[e + q, :, d:d + rows_out].reshape(frames * rows_out * PITCH, chans)
                rhs = jnp.concatenate([w2[1, d, e], w2[0, d, e]], 0)
                term = dot_nt(lhs, rhs)
                acc = term if acc is None else acc + term
        acc = acc.reshape(frames, rows_out // 2, 2, PITCH, 2 * c3)
        v0 = acc[0, ..., c3:] + acc[1, ..., :c3]
        v1 = acc[1, ..., c3:]
        for o, v in enumerate((v0, v1)):
            part2[q, o] = jnp.concatenate([v[:, 1], v[:, 0]], -1)

    tall3, wide3 = third.shape[1:3]
    shift = 2 * 128

    def put3(f, row, col, value):
        n = value.shape[0]
        e3[f, row, col:col + n, 0:c3] = value

    for f in range(frames):
        for r in range(tall3):
            put3(f, r + 1, off, read(third, f, r))
        for j in range(2):
            half = wide3 // 2
            put3(f, 0, off + j * half, read(up2, f, j)[:, shift:shift + c3] * top)
            put3(f, tall3 + 1, off + j * half, read(down2, f, j)[:, shift:shift + c3] * bottom)
        for r in range(tall3 // 2):
            pa = at_side(side_a, f, r)[:, shift:shift + c3]
            pb = at_side(side_b, f, r)[:, shift:shift + c3]
            vl = pa * left[0] + pb * left[1]
            vr = pa * right[0] + pb * right[1]
            for j in range(2):
                put3(f, 1 + 2 * r + j, off - 1, vl[j:j + 1])
                put3(f, 1 + 2 * r + j, off + wide3, vr[j:j + 1])
        for row, da, db, s in ((0, dau, dbu, top), (tall3 + 1, dad, dbd, bottom)):
            pa = at_corner(da, f, 0)[0:1, shift:shift + c3]
            pb = at_corner(db, f, 0)[0:1, shift:shift + c3]
            put3(f, row, off - 1, pa * (left[0] * s) + pb * (left[1] * s))
            put3(f, row, off + wide3, pa * (right[0] * s) + pb * (right[1] * s))
    height, width = tall3 // 4, wide3 // 4
    lanes = lax.broadcasted_iota(jnp.int32, (width, 128), 1)
    for k in range(6):
        for f in range(frames):
            for r in range(tall3 + 2):
                value = e3[f, r, pl.ds(off - 1 + k, width, stride=4), :]
                xc3[k, f, r // 4, r % 4] = jnp.where(lanes < c3, value, 0.0).astype(BF16)
    acc = None
    for j in range(6):
        for k in range(0, 6, 2):
            lhs = jnp.concatenate(
                [
                    xc3[kk, :, j // 4:j // 4 + height, j % 4].reshape(frames * height * width, 128)
                    for kk in (k, k + 1)
                ],
                -1,
            )
            base = (j * 6 + k) * 128
            rhs = jnp.concatenate([w3c[base:base + 128], w3c[base + 128:base + 256]], -1)
            term = dot_nt(lhs, rhs)
            acc = term if acc is None else acc + term
    size = height * width
    part3[0] = acc[:size, 64:] + acc[size:, :64]
    part3[1] = acc[size:, 64:]


def normed(values, gain, total):
    meansq = jnp.sum(values * values, axis=-1, keepdims=True) * (1.0 / total)
    out = values * lax.rsqrt(meansq + EPS) * gain
    return out / (1.0 + jnp.exp(-out))


def frames_kernel(
    count, feats, cache, up1, down1, side_a, side_b, dau, dbu, dad, dbd, w1, g1, g2, g3,
    part2, part3, wc2, wc3, spread_ref,
    out,
    e1, x1, e2, x2, x3,
):
    flags = position(count)
    top, bottom, left, right = sides(flags)
    frames, height, width, chans = feats.shape
    old = cache.shape[0]
    total = frames + old
    c2 = g2.shape[0]
    c3 = c2 // 2
    read = lambda ref, *ix: ref[ix].astype(F32)

    off = 8
    rows1, rows2 = height + 2, height + 1
    lanes2 = e2.shape[-1]
    always = flags[2] + flags[3] > 0

    cols = lax.broadcasted_iota(jnp.int32, (PITCH, c2), 0)
    first = 1 - flags[2]
    last = width + flags[3]
    inside = (cols >= first) & (cols <= last)
    at_top = inside & (cols < flags[0] * PITCH)
    at_bottom = inside & (cols < flags[1] * PITCH)

    @pl.when(always)
    def _():
        for f in range(total):
            for r in range(height + 4):
                if r < 2:
                    own = read(up1, f, r) * top
                    pa, pb, s = read(dau, 2 * f + r), read(dbu, 2 * f + r), top
                elif r < height + 2:
                    own = read(cache, f, r - 2) if f < old else read(feats, f - old, r - 2)
                    pa, pb, s = read(side_a, f * height + r - 2), read(side_b, f * height + r - 2), 1.0
                else:
                    own = read(down1, f, r - height - 2) * bottom
                    at = 2 * f + r - height - 2
                    pa, pb, s = read(dad, at), read(dbd, at), bottom
                e1[f, r, off:off + width, :] = own
                e1[f, r, off - 2:off, :] = pa * (left[0] * s) + pb * (left[1] * s)
                e1[f, r, off + width:off + width + 2, :] = pa * (right[0] * s) + pb * (right[1] * s)
        gain = g1[...].reshape(1, chans)
        for f in range(old, total):
            for r in range(height + 4):
                e1[f, r] = normed(e1[f, r], gain, chans)
        for k in range(3):
            for f in range(total):
                for r in range(height + 4):
                    x1[k, f, r] = e1[f, r, off - 2 + k:off - 2 + k + PITCH, :].astype(BF16)

    @pl.when(always)
    def _():
        pieces = [
            (t, d, e, slice(i, i + 128))
            for t in range(3) for d in range(3) for e in range(3) for i in range(0, chans, 128)
        ]
        half = frames // 2
        accs = [None, None]
        for i in range(0, len(pieces), 4):
            rhs = jnp.concatenate([w1[t, d, e, :, ch] for t, d, e, ch in pieces[i:i + 4]], -1)
            for h in range(2):
                lhs = [
                    x1[e, t + h * half:t + h * half + half, d:d + rows1, :, ch].reshape(-1, 128)
                    for t, d, e, ch in pieces[i:i + 4]
                ]
                term = dot_nt(jnp.concatenate(lhs, -1), rhs)
                accs[h] = term if accs[h] is None else accs[h] + term
        accs = [v.reshape(half, rows1, PITCH, c2) for v in accs]

        gain = g2[...].reshape(1, c2)
        e2[:, :, :, c2:lanes2] = jnp.zeros(e2.shape[:3] + (lanes2 - c2,), F32)
        for f in range(frames):
            for r in range(rows1):
                keep = at_top if r == 0 else at_bottom if r == rows1 - 1 else inside
                value = jnp.where(keep, accs[f // half][f % half, r].astype(BF16).astype(F32), 0.0)
                e2[f, r, off:off + PITCH, 0:c2] = normed(value, gain, c2)
        for k in range(3):
            for f in range(frames):
                for r in range(rows1):
                    x2[k, f, r] = e2[f, r, off - 1 + k:off - 1 + k + PITCH, :].astype(BF16)

    @pl.when(always)
    def _():
        lanes = lax.broadcasted_iota(jnp.int32, (PITCH, c2), 1)
        lower = lanes < c3
        gain = jnp.concatenate([g3[...].reshape(1, c3)] * 2, -1)
        every = ([], [])
        for t in range(3):
            count = frames - (2 - t)
            accs = [None, None]
            for rs in range(2):
                for q in range(2):
                    lhs = [
                        x2[q + cs, 0:count, rs:rs + rows2].reshape(count * rows2 * PITCH, lanes2)
                        for cs in range(2)
                    ]
                    base = ((t * 2 + q) * 2 + rs) * 2
                    term = dot_nt(jnp.concatenate(lhs, -1), jnp.concatenate([wc2[base], wc2[base + 1]], -1))
                    accs[q] = term if accs[q] is None else accs[q] + term
            for q in range(2):
                every[q].append(accs[q].reshape(count, rows2, PITCH, c2))
        for q in range(2):
            parts = every[q]
            for f in range(frames):
                for r in range(rows2):
                    value = parts[2][f, r]
                    if f >= 1:
                        value = value + parts[1][f - 1, r]
                    if f >= 2:
                        value = value + parts[0][f - 2, r]
                    else:
                        value = value + part2[q, f, r]
                    keep = inside
                    if r == 0:
                        keep = (lower & inside) | at_top
                    if r == rows2 - 1:
                        keep = (~lower & inside) | at_bottom
                    value = jnp.where(keep, value.astype(BF16).astype(F32), 0.0)
                    square = value * value
                    sum_low = jnp.sum(jnp.where(lower, square, 0.0), axis=-1, keepdims=True)
                    sum_high = jnp.sum(jnp.where(lower, 0.0, square), axis=-1, keepdims=True)
                    scale = jnp.where(
                        lower,
                        lax.rsqrt(sum_low * (1.0 / c3) + EPS),
                        lax.rsqrt(sum_high * (1.0 / c3) + EPS),
                    )
                    value = value * scale * gain
                    e2[f, r, off:off + PITCH, 0:c2] = value / (1.0 + jnp.exp(-value))
            for f in range(frames):
                for r in range(rows2):
                    for cs in ((1, 3) if q == 0 else (0, 2)):
                        start = off + (0, 1, 1, 2)[cs]
                        x3[cs, f, r] = e2[f, r, start:start + width, :].astype(BF16)

    @pl.when(always)
    def _():
        acc = None
        for rs in range(2):
            for cs in (0, 2):
                lhs = [
                    x3[i, :, rs:rs + height].reshape(frames * height * width, lanes2) for i in (cs, cs + 1)
                ]
                base = (rs * 4 + cs) * 192
                rhs = [wc3[base:base + 192], wc3[base + 192:base + 384]]
                term = dot_nt(jnp.concatenate(lhs, -1), jnp.concatenate(rhs, -1))
                acc = term if acc is None else acc + term
        size = height * width
        acc = acc.reshape(frames, size, 192)
        turned = []
        for f in range(frames):
            value = acc[f, :, 0:64]
            if f >= 1:
                value = value + acc[f - 1, :, 64:128]
            value = value + (acc[f - 2, :, 128:192] if f >= 2 else part3[f])
            value = value.T
            turned.append(jnp.concatenate([value[b * 16:(b + 1) * 16] for b in range(4)], -1))
        turned = jnp.concatenate(turned, 0)
        result = None
        for _ in range(3):
            piece = turned.astype(BF16)
            turned = turned - piece.astype(F32)
            term = jnp.dot(piece, spread_ref[...], preferred_element_type=F32)
            result = term if result is None else result + term
        for f in range(frames):
            for c in range(out.shape[1]):
                for r in range(height):
                    out[f, c, 4 * r:4 * r + 4, :] = result[
                        f * 16 + c * 4:f * 16 + c * 4 + 4, r * 4 * width:(r + 1) * 4 * width
                    ]


def body(count, features, cache_first, cache_second, cache_third, w1, w2, w3, g1, g2, g3):
    tile_rows = count // TILES_X
    last_dims = lambda v: v[:, :, 0].transpose(0, 2, 3, 1)
    feats, old1, old2, old3 = map(last_dims, (features, cache_first, cache_second, cache_third))
    frames, height, width, c1 = feats.shape
    old = old1.shape[0]
    total = frames + old
    c2, c3 = old2.shape[-1], old3.shape[-1]
    rgb = w3.shape[3]
    row_pairs = [0] if tile_rows <= 2 else [0, 1]
    vmem = pl.BlockSpec(memory_space=pltpu.VMEM)
    bf = lambda *shape: jax.ShapeDtypeStruct(shape, BF16)

    def call(kernel, ins, outs, scratch, limit, flops, space=vmem):
        return pl.pallas_call(
            kernel,
            out_shape=outs,
            in_specs=[space] * len(ins),
            out_specs=[vmem] * len(outs),
            scratch_shapes=scratch,
            compiler_params=pltpu.CompilerParams(vmem_limit_bytes=int(limit * 2**20)),
            cost_estimate=pl.CostEstimate(flops=flops, bytes_accessed=2_000_000, transcendentals=0),
        )(*ins)

    side = bf(total * height + old * 2 * height, 2, c1)
    corner = bf(total * 2 + old * 2, 2, c1)
    rows = [bf(old, 2, 2 * width, c1), bf(total, 2, width, c1)]
    packed = call(
        functools.partial(pack_kernel, count, row_pairs), (feats, old1, old2, old3),
        [side] * 2 + (rows + [corner] * 2) * len(row_pairs),
        [
            pltpu.VMEM(feats.shape, BF16),
            pltpu.VMEM(old1.shape, BF16),
            pltpu.VMEM(old2.shape, BF16),
            pltpu.VMEM((old, 2, 4 * width, c3), BF16),
            pltpu.VMEM((old, 4 * height, 8, c3), BF16),
            pltpu.VMEM((old, 4 * height, 8, c3), BF16),
            pltpu.SemaphoreType.DMA((7,)),
        ],
        62.9, 100_000_000, pl.BlockSpec(memory_space=pltpu.HBM),
    )

    sent = [swap(packed[cp], count, None, cp) for cp in (0, 1)]
    rows1, rows2, corners = [], [], ([], [])
    for i, rp in enumerate(row_pairs):
        piece = packed[2 + 4 * i:6 + 4 * i]
        rows2.append(swap(piece[0], count, rp, None))
        for cp in (0, 1):
            corners[cp].append(swap(piece[2 + cp], count, rp, cp))
        rows1.append(swap(piece[1], count, rp, None))
    odd_row = (lax.axis_index("tile") + TILES_X // 2) // TILES_X % 2 == 1

    def above(pieces):
        return pieces[0] if len(pieces) == 1 else jnp.where(odd_row, pieces[0], pieces[1])

    def below(pieces):
        return pieces[0] if len(pieces) == 1 else jnp.where(odd_row, pieces[1], pieces[0])

    diagonals = [pick(corners[cp]) for pick in (above, below) for cp in (0, 1)]
    size = height * width
    wc2, wc3, w3c = call(
        weights_kernel,
        (w2, w3, jnp.asarray(fine_taps(rgb), BF16), jnp.asarray(cache_taps(rgb), BF16)),
        [bf(24, 2 * c3, 256), bf(8 * 192, 256), bf(36 * 128, 128)],
        [pltpu.VMEM((192, 192), F32)], 16, 500_000_000,
    )
    part2, part3 = call(
        functools.partial(history_kernel, count),
        (old2, old3, above(rows2), below(rows2), *sent, *diagonals, w2, w3c),
        [
            jax.ShapeDtypeStruct((2, 2, height + 1, PITCH, c2), F32),
            jax.ShapeDtypeStruct((2, size, 64), F32),
        ],
        [
            pltpu.VMEM((old, 2 * height + 4, 64, 128), F32),
            pltpu.VMEM((old, 2 * height + 4, 64, 128), F32),
            pltpu.VMEM((old, 4 * height + 2, 96, 128), F32),
            pltpu.VMEM((4, old, 2 * height + 4, PITCH, c2), BF16),
            pltpu.VMEM((6, old, height + 1, 4, width, 128), BF16),
        ],
        22, 4_000_000_000,
    )
    (out,) = call(
        functools.partial(frames_kernel, count),
        (
            feats, old1, above(rows1), below(rows1), *sent, *diagonals, w1, g1, g2, g3,
            part2, part3, wc2, wc3, jnp.asarray(spread(height, width), BF16),
        ),
        [jax.ShapeDtypeStruct((frames, rgb, 4 * height, 4 * width), F32)],
        [
            pltpu.VMEM((total, height + 4, 40, c1), F32),
            pltpu.VMEM((3, total, height + 4, PITCH, c1), BF16),
            pltpu.VMEM((frames, height + 2, 40, 256), F32),
            pltpu.VMEM((3, frames, height + 2, PITCH, 256), BF16),
            pltpu.VMEM((4, frames, height + 1, width, 256), BF16),
        ],
        26, 10_000_000_000,
    )
    return out[:, :, None]


def solution(mesh):
    tiled = P("groups", None, "tile", None, None)
    return jax.shard_map(
        functools.partial(body, mesh.shape["tile"]),
        mesh=mesh,
        in_specs=(tiled,) * 4 + (P(),) * 6,
        out_specs=tiled,
        check_vma=False,
    )
```

time: 63.4 us -> 41.4 us (0.65)
  Pallas kernels: 30.9 us -> 19.8 us
  other arithmetic: 10.5 us -> 0 us
  local copies, waits for them, and re-layouts: 7.44 us -> 2.65 us
  waiting for transfers between devices: 0.02 us -> 4.56 us
    pallas_call x2 -> x4, Pallas kernels: 30.9 us -> 19.8 us  [call(): pl.pallas_call(kernel, out_shape=outs, in_specs=[space] * len(ins), out_s...]
    select_n x12 -> x0, other arithmetic: 7.79 us -> none  [edge(): return jnp.where(last, tail, head)]
    slice x8 -> x0, local copies, waits for them, and re-layouts: 5.09 us -> none  [the longest x2 1.37 us: body(): sent[cp][:cut_side].reshape(frames + old, height, 2, -1)]
    ppermute x6, waiting for transfers between devices: 0.02 us -> 4.56 us  [swap(): return lax.ppermute(values, 'tile', pairs_of(count, row_pair, col_pair))]
    concatenate x10 -> x0, other arithmetic: 2.2 us -> none  [the longest x1 0.75 us: body(): jnp.concatenate([jnp.pad(flat3, ((0, 0), (0, 192 - c3))), jnp.pad(flat3,...]
    unnamed x13 -> x30, local copies, waits for them, and re-layouts: 1.32 us -> 2.65 us
  transfers between devices with their start and end apart: 6 -> 6, of which waited for: 0 -> 1; matrix products, arithmetic and copies ran while one was open for 20% -> 0% of each run, Pallas kernels for 13% -> 11%
where the time goes in v1:
time: 41.4 us; the launch traced here: 41.1 us
  Pallas kernels  19.8 us (48%)
  starting transfers between devices  13.8 us (33%)
  waiting for transfers between devices  4.56 us (11%)
  local copies, waits for them, and re-layouts  2.65 us (6%)
    pallas_call x4, Pallas kernels, call(): pl.pallas_call(kernel, out_shape=outs, in_specs=[space] * len(ins), out_s...  19.8 us
    ppermute x6, starting transfers between devices, swap(): return lax.ppermute(values, 'tile', pairs_of(count, row_pair, col_pair))  13.8 us
    ppermute x6, waiting for transfers between devices, swap(): return lax.ppermute(values, 'tile', pairs_of(count, row_pair, col_pair))  4.56 us
    unnamed x30, local copies, waits for them, and re-layouts  2.65 us
  transfers between devices with their start and end apart: 6, of which 1 were waited for; matrix products, arithmetic and copies ran while one was open for 0% of the time, Pallas kernels for 11%

profile of v1, /device:TPU:0, one launch (start us, length us, event | category | flops | bytes accessed | tf_op | source)
XLA Modules:
  0.0 41.1 jit_solution(4124335522808495783)
XLA Ops:
  0.0 0.0 copy-start.4
  0.0 0.0 copy-start.8
  0.0 2.5 %shard_map.127 = (bf16[80,2,384]{2,1,0:T(2,128)(2,1)}, bf16[80,2,384]{2,1,0:T(2,128)(2,1)}, bf16[2,2,32,384]{3,2,1,0:T(8,128)(2,1)}, bf16[6,2,16,384]{3,2,1,0:T(...) custom-call(bf16[4,8,16,384]{3,2,1,0:T(8,128)(2,1)} %bitcast.19, bf16[2,8,16,384]{3,2,1,0:T(8,128)(2,1)} %bitcast.21, ...), custom_call_target="tpu_custom_call" | custom-call | flops 100000000 | bytes 2000000 | tf_op jit(solution)/shard_map/pallas_call | solution.py:515
  2.5 0.6 %collective-permute-start.1 = (bf16[80,2,384]{2,1,0:T(2,128)(2,1)}, bf16[80,2,384]{2,1,0:T(2,128)(2,1)S(1)}, u32[]{:S(2)}, u32[]{:S(2)}) collective-permute-start(bf16[80,2,384]{2,1,0:T(2,128)(2,1)} %get-tuple-element.17), channel_id=1, source_target_pairs={{0,1},{1,0},{2,3},{3,2},{4,5},{5,4},{6,7},{7,6},{8,9},{9,8},{10,11... | collective-permute-start | bytes 368648 | tf_op jit(solution)/shard_map/ppermute | solution.py:39
  3.1 7.5 %collective-permute-start.2 = (bf16[80,2,384]{2,1,0:T(2,128)(2,1)}, bf16[80,2,384]{2,1,0:T(2,128)(2,1)S(1)}, u32[]{:S(2)}, u32[]{:S(2)}) collective-permute-start(bf16[80,2,384]{2,1,0:T(2,128)(2,1)} %get-tuple-element.18), channel_id=1, source_target_pairs={{0,15},{1,2},{2,1},{3,3},{4,4},{5,6},{6,5},{7,8},{8,7},{9,10},{10,... | collective-permute-start | bytes 368648 | tf_op jit(solution)/shard_map/ppermute | solution.py:39
  10.6 0.1 collective-permute-start.5
  10.7 0.1 collective-permute-start.3
  10.8 2.9 %collective-permute-start.4 = (bf16[16,2,384]{2,1,0:T(2,128)(2,1)}, bf16[16,2,384]{2,1,0:T(2,128)(2,1)S(1)}, u32[]{:S(2)}, u32[]{:S(2)}) collective-permute-start(bf16[16,2,384]{2,1,0:T(2,128)(2,1)} %get-tuple-element.20), channel_id=1, source_target_pairs={{0,7},{1,10},{2,9},{3,3},{4,4},{5,14},{6,13},{7,0},{8,15},{9,2},{1... | collective-permute-start | bytes 73736 | tf_op jit(solution)/shard_map/ppermute | solution.py:39
  13.7 0.0 copy-done.4
  13.7 0.0 copy-done.8
  13.8 0.0 copy-start
  13.8 1.3 %copy-done = bf16[3,3,3,96,192]{4,3,2,1,0:T(8,128)(2,1)S(1)} copy-done((bf16[3,3,3,96,192]{4,3,2,1,0:T(8,128)(2,1)S(1)}, bf16[3,3,3,96,192]{4,3,2,1,0:T(8,128)(2,1)}, u32[]{:S(2)}) %copy-start) | copy-done | bytes 995352
  15.1 0.0 copy-start.2
  15.1 1.3 %copy-done.2 = bf16[4608,96]{1,0:T(8,128)(2,1)S(1)} copy-done((bf16[4608,96]{1,0:T(8,128)(2,1)S(1)}, bf16[4608,96]{1,0:T(8,128)(2,1)}, u32[]{:S(2)}) %copy-start.2) | copy-done | bytes 884760
  16.4 0.0 copy-start.14
  16.4 0.0 copy-start.1
  16.4 0.0 copy-start.3
  16.4 0.0 copy-start.5
  16.4 1.3 %shard_map.128 = (bf16[24,192,256]{2,1,0:T(8,128)(2,1)S(1)}, bf16[1536,256]{1,0:T(8,128)(2,1)S(1)}, bf16[4608,128]{1,0:T(8,128)(2,1)S(1)}) custom-call(bf16[3,3,3,96,192]{4,3,2,1,0:T(8,128)(2,1)S(1)} %copy-done, bf16[3,3,3,3,96]{4,3,2,1,0:T(4,128)(2,1)S(1)} %copy-done.8, bf16[1536,192]{1,0:T(8,128)(2,1)S(1)} %copy-done.4, bf16[4608,96]{1,0:T(8,128)(2,1)S(1)} %copy-done.2), custom_call_target="tpu_custom_call" | custom-call | flops 500000000 | bytes 2000000 | tf_op jit(solution)/shard_map/pallas_call | solution.py:515
  17.7 0.0 collective-permute-done.3.dau.dad
  17.7 0.0 copy-done.14
  17.7 2.7 %collective-permute-start = (bf16[6,2,16,384]{3,2,1,0:T(8,128)(2,1)S(1)}, bf16[6,2,16,384]{3,2,1,0:T(8,128)(2,1)S(1)}, u32[]{:S(2)}, u32[]{:S(2)}) collective-permute-start(bf16[6,2,16,384]{3,2,1,0:T(8,128)(2,1)S(1)} %copy-done.14), channel_id=1, source_target_pairs={{0,8},{1,9},{2,10},{3,11},{4,12},{5,13},{6,14},{7,15},{8,0},{9,1},... | collective-permute-start | bytes 442376 | tf_op jit(solution)/shard_map/ppermute | solution.py:39
  20.3 0.0 collective-permute-done.4.dbu.dbd
  20.3 0.0 collective-permute-done.5.up2.down2
  20.4 0.0 collective-permute-done.1.side_a
  20.4 0.0 collective-permute-done.2.side_b
  20.4 0.0 copy-done.1
  20.4 0.0 copy-done.3
  20.4 0.0 copy-done.5
  20.4 0.0 copy-start.6
  20.4 0.0 copy-start.7
  20.4 0.0 copy-start.9
  20.4 0.0 copy-start.10
  20.4 0.0 copy-start.11
  20.5 0.0 copy-start.12
  20.5 0.0 copy-start.13
  20.5 3.3 %shard_map.129 = (f32[2,2,9,24,192]{4,3,2,1,0:T(8,128)S(1)}, f32[2,128,64]{2,1,0:T(8,128)S(1)}) custom-call(bf16[2,16,32,192]{3,2,1,0:T(8,128)(2,1)S(1)} %bitcast.18, bf16[2,32,64,96]{3,2,1,0:T(8,128)(2,1)S(1)} %bitcast.16, bf16[2,2,32,384]{3,2,1,0:T(8,128)(2,1)S(1)} %collective-permute-done.5.up2.down2, ...), custom_call_target="tpu_custom_call" | custom-call | flops 4000000000 | bytes 2000000 | tf_op jit(solution)/shard_map/pallas_call | solution.py:515
  23.8 4.5 %collective-permute-done.up1.down1 = bf16[6,2,16,384]{3,2,1,0:T(8,128)(2,1)S(1)} collective-permute-done((bf16[6,2,16,384]{3,2,1,0:T(8,128)(2,1)S(1)}, bf16[6,2,16,384]{3,2,1,0:T(8,128)(2,1)S(1)}, u32[]{:S(2)}, u32[]{:S(2)}) %collective-permute-start) | collective-permute-done | bytes 147488 | tf_op jit(solution)/shard_map/ppermute | solution.py:39
  28.4 0.0 copy-done.6
  28.4 0.0 copy-done.7
  28.4 0.0 copy-done.9
  28.4 0.0 copy-done.10
  28.4 0.0 copy-done.11
  28.4 0.0 copy-done.12
  28.4 0.0 copy-done.13
  28.4 12.7 %shard_map.130 = f32[4,3,32,64]{3,2,1,0:T(8,128)} custom-call(bf16[4,8,16,384]{3,2,1,0:T(8,128)(2,1)S(1)} %bitcast.20, bf16[2,8,16,384]{3,2,1,0:T(8,128)(2,1)S(1)} %bitcast.22, bf16[6,2,16,384]{3,2,1,0:T(8,128)(2,1)S(1)} %collective-permute-done.up1.down1, bf16[6,2,16,384]{3,2,1,0:T(8,128)(2,1)S(1)} %collective-permute-done.up1.down1, ...), custom_call_target="tpu_custom_call" | custom-call | flops 10000000000 | bytes 2000000 | tf_op jit(solution)/shard_map/pallas_call | solution.py:515
Async XLA Ops:
  0.0 13.7 %copy-start.4 = (bf16[1536,192]{1,0:T(8,128)(2,1)S(1)}, bf16[1536,192]{1,0:T(8,128)(2,1)}, u32[]{:S(2)}) copy-start(bf16[1536,192]{1,0:T(8,128)(2,1)} %constant.6.clone.taps3) | copy-start | bytes 1769476
  0.0 13.7 %copy-start.8 = (bf16[3,3,3,3,96]{4,3,2,1,0:T(4,128)(2,1)S(1)}, bf16[3,3,3,3,96]{4,3,2,1,0:T(4,128)(2,1)}, u32[]{:S(2)}) copy-start(bf16[3,3,3,3,96]{4,3,2,1,0:T(4,128)(2,1)} %w3.1) | copy-start | bytes 46660
  2.5 17.8 %collective-permute-start.1 = (bf16[80,2,384]{2,1,0:T(2,128)(2,1)}, bf16[80,2,384]{2,1,0:T(2,128)(2,1)S(1)}, u32[]{:S(2)}, u32[]{:S(2)}) collective-permute-start(bf16[80,2,384]{2,1,0:T(2,128)(2,1)} %get-tuple-element.17), channel_id=1, source_target_pairs={{0,1},{1,0},{2,3},{3,2},{4,5},{5,4},{6,7},{7,6},{8,9},{9,8},{10,11... | collective-permute-start | bytes 368648 | tf_op jit(solution)/shard_map/ppermute | solution.py:39
  3.1 17.3 %collective-permute-start.2 = (bf16[80,2,384]{2,1,0:T(2,128)(2,1)}, bf16[80,2,384]{2,1,0:T(2,128)(2,1)S(1)}, u32[]{:S(2)}, u32[]{:S(2)}) collective-permute-start(bf16[80,2,384]{2,1,0:T(2,128)(2,1)} %get-tuple-element.18), channel_id=1, source_target_pairs={{0,15},{1,2},{2,1},{3,3},{4,4},{5,6},{6,5},{7,8},{8,7},{9,10},{10,... | collective-permute-start | bytes 368648 | tf_op jit(solution)/shard_map/ppermute | solution.py:39
  10.6 9.7 %collective-permute-start.5 = (bf16[2,2,32,384]{3,2,1,0:T(8,128)(2,1)}, bf16[2,2,32,384]{3,2,1,0:T(8,128)(2,1)S(1)}, u32[]{:S(2)}, u32[]{:S(2)}) collective-permute-start(bf16[2,2,32,384]{3,2,1,0:T(8,128)(2,1)} %get-tuple-element.21), channel_id=1, source_target_pairs={{0,8},{1,9},{2,10},{3,11},{4,12},{5,13},{6,14},{7,15},{8,0},{9,1},... | collective-permute-start | bytes 294920 | tf_op jit(solution)/shard_map/ppermute | solution.py:39
  10.7 6.9 %collective-permute-start.3 = (bf16[16,2,384]{2,1,0:T(2,128)(2,1)}, bf16[16,2,384]{2,1,0:T(2,128)(2,1)S(1)}, u32[]{:S(2)}, u32[]{:S(2)}) collective-permute-start(bf16[16,2,384]{2,1,0:T(2,128)(2,1)} %get-tuple-element.19), channel_id=1, source_target_pairs={{0,9},{1,8},{2,11},{3,10},{4,13},{5,12},{6,15},{7,14},{8,1},{9,0},... | collective-permute-start | bytes 73736 | tf_op jit(solution)/shard_map/ppermute | solution.py:39
  10.8 9.5 %collective-permute-start.4 = (bf16[16,2,384]{2,1,0:T(2,128)(2,1)}, bf16[16,2,384]{2,1,0:T(2,128)(2,1)S(1)}, u32[]{:S(2)}, u32[]{:S(2)}) collective-permute-start(bf16[16,2,384]{2,1,0:T(2,128)(2,1)} %get-tuple-element.20), channel_id=1, source_target_pairs={{0,7},{1,10},{2,9},{3,3},{4,4},{5,14},{6,13},{7,0},{8,15},{9,2},{1... | collective-permute-start | bytes 73736 | tf_op jit(solution)/shard_map/ppermute | solution.py:39
  13.8 1.3 %copy-start = (bf16[3,3,3,96,192]{4,3,2,1,0:T(8,128)(2,1)S(1)}, bf16[3,3,3,96,192]{4,3,2,1,0:T(8,128)(2,1)}, u32[]{:S(2)}) copy-start(bf16[3,3,3,96,192]{4,3,2,1,0:T(8,128)(2,1)} %w2.3) | copy-start | bytes 2985988
  15.1 1.3 %copy-start.2 = (bf16[4608,96]{1,0:T(8,128)(2,1)S(1)}, bf16[4608,96]{1,0:T(8,128)(2,1)}, u32[]{:S(2)}) copy-start(bf16[4608,96]{1,0:T(8,128)(2,1)} %constant.7.clone.taps3c) | copy-start | bytes 2654212
  16.4 1.3 %copy-start.14 = (bf16[6,2,16,384]{3,2,1,0:T(8,128)(2,1)S(1)}, bf16[6,2,16,384]{3,2,1,0:T(8,128)(2,1)}, u32[]{:S(2)}) copy-start(bf16[6,2,16,384]{3,2,1,0:T(8,128)(2,1)} %get-tuple-element.16) | copy-start | bytes 442372
  16.4 4.0 %copy-start.1 = (bf16[3,3,3,96,192]{4,3,2,1,0:T(8,128)(2,1)S(1)}, bf16[3,3,3,96,192]{4,3,2,1,0:T(8,128)(2,1)}, u32[]{:S(2)}) copy-start(bf16[3,3,3,96,192]{4,3,2,1,0:T(8,128)(2,1)} %w2.3) | copy-start | bytes 2985988
  16.4 4.0 %copy-start.3 = (bf16[2,96,1,32,64]{1,4,3,2,0:T(8,128)(2,1)S(1)}, bf16[2,96,1,32,64]{1,4,3,2,0:T(8,128)(2,1)}, u32[]{:S(2)}) copy-start(bf16[2,96,1,32,64]{1,4,3,2,0:T(8,128)(2,1)} %param.16) | copy-start | bytes 2359300
  16.4 4.0 %copy-start.5 = (bf16[2,192,1,16,32]{1,4,3,2,0:T(8,128)(2,1)S(1)}, bf16[2,192,1,16,32]{1,4,3,2,0:T(8,128)(2,1)}, u32[]{:S(2)}) copy-start(bf16[2,192,1,16,32]{1,4,3,2,0:T(8,128)(2,1)} %param.15) | copy-start | bytes 1179652
  17.7 10.7 %collective-permute-start = (bf16[6,2,16,384]{3,2,1,0:T(8,128)(2,1)S(1)}, bf16[6,2,16,384]{3,2,1,0:T(8,128)(2,1)S(1)}, u32[]{:S(2)}, u32[]{:S(2)}) collective-permute-start(bf16[6,2,16,384]{3,2,1,0:T(8,128)(2,1)S(1)} %copy-done.14), channel_id=1, source_target_pairs={{0,8},{1,9},{2,10},{3,11},{4,12},{5,13},{6,14},{7,15},{8,0},{9,1},... | collective-permute-start | bytes 442376 | tf_op jit(solution)/shard_map/ppermute | solution.py:39
  20.4 8.0 %copy-start.6 = (bf16[4,384,1,8,16]{1,4,3,2,0:T(8,128)(2,1)S(1)}, bf16[4,384,1,8,16]{1,4,3,2,0:T(8,128)(2,1)}, u32[]{:S(2)}) copy-start(bf16[4,384,1,8,16]{1,4,3,2,0:T(8,128)(2,1)} %param.13) | copy-start | bytes 1179652
  20.4 8.0 %copy-start.7 = (bf16[2,384,1,8,16]{1,4,3,2,0:T(8,128)(2,1)S(1)}, bf16[2,384,1,8,16]{1,4,3,2,0:T(8,128)(2,1)}, u32[]{:S(2)}) copy-start(bf16[2,384,1,8,16]{1,4,3,2,0:T(8,128)(2,1)} %param.14) | copy-start | bytes 589828
  20.4 8.0 %copy-start.9 = (bf16[3,3,3,192,384]{4,3,2,1,0:T(8,128)(2,1)S(1)}, bf16[3,3,3,192,384]{4,3,2,1,0:T(8,128)(2,1)}, u32[]{:S(2)}) copy-start(bf16[3,3,3,192,384]{4,3,2,1,0:T(8,128)(2,1)} %w1.1) | copy-start | bytes 11943940
  20.4 7.9 %copy-start.10 = (f32[384]{0:T(512)S(1)}, f32[384]{0:T(512)}, u32[]{:S(2)}) copy-start(f32[384]{0:T(512)} %g1.1) | copy-start | bytes 4612
  20.4 7.9 %copy-start.11 = (f32[192]{0:T(256)S(1)}, f32[192]{0:T(256)}, u32[]{:S(2)}) copy-start(f32[192]{0:T(256)} %g2.1) | copy-start | bytes 2308
  20.5 7.9 %copy-start.12 = (f32[96]{0:T(128)S(1)}, f32[96]{0:T(128)}, u32[]{:S(2)}) copy-start(f32[96]{0:T(128)} %g3.1) | copy-start | bytes 1156
  20.5 7.9 %copy-start.13 = (bf16[512,512]{1,0:T(8,128)(2,1)S(1)}, bf16[512,512]{1,0:T(8,128)(2,1)}, u32[]{:S(2)}) copy-start(bf16[512,512]{1,0:T(8,128)(2,1)} %constant.8.clone.spread_ref) | copy-start | bytes 1572868

commit v2 on v1

--- a/solution.py
+++ b/solution.py
@@ -2,7 +2,6 @@
 
 import jax
 import jax.numpy as jnp
-import numpy as np
 from jax import lax
 from jax.experimental import pallas as pl
 from jax.experimental.pallas import tpu as pltpu
@@ -37,47 +36,6 @@
 
 def swap(values, count, row_pair, col_pair):
     return lax.ppermute(values, "tile", pairs_of(count, row_pair, col_pair))
-
-
-@functools.lru_cache
-def fine_taps(rgb):
-    slots = np.zeros((2, 4, 3, 4, 4, 4, 2, 3, 3, 3, rgb), np.float32)
-    for a in range(4):
-        for d in range(3):
-            row = (a + d - 1) // 2
-            rs, half = {-1: (0, 1), 0: (0, 0), 1: (1, 1), 2: (1, 0)}[row]
-            for b in range(4):
-                for e in range(3):
-                    cs = (b + e - 1) // 2 + 1
-                    for t in range(3):
-                        for c in range(rgb):
-                            slots[rs, cs, 2 - t, b, c, a, half, t, d, e, c] += 1
-    flat = slots.reshape(8 * 192, 2, 27 * rgb)
-    return np.pad(flat, ((0, 0), (0, 0), (0, 96 - 27 * rgb))).reshape(8 * 192, 192)
-
-
-@functools.lru_cache
-def cache_taps(rgb):
-    slots = np.zeros((6, 6, 2, 4, 4, 4, 3, 3, 3, rgb), np.float32)
-    for a in range(4):
-        for d in range(3):
-            for b in range(4):
-                for e in range(3):
-                    for t in range(2):
-                        for c in range(rgb):
-                            slots[a + d, b + e, 1 - t, b, c, a, t, d, e, c] += 1
-    flat = slots.reshape(36 * 128, 27 * rgb)
-    return np.pad(flat, ((0, 0), (0, 96 - 27 * rgb)))
-
-
-@functools.lru_cache
-def spread(height, width):
-    out = np.zeros((4, height, width, height, width, 4), np.float32)
-    for b in range(4):
-        for r in range(height):
-            for c in range(width):
-                out[b, r, c, r, c, b] = 1
-    return out.reshape(4 * height * width, 4 * height * width)
 
 
 def dot_nt(lhs, rhs):
@@ -172,20 +130,46 @@
                         side[at + r, :, aside] = jnp.concatenate(pair, 0).astype(BF16)
 
 
-def weights_kernel(w2, w3, taps3, taps3c, wc2, wc3, w3c, flat):
-    c3 = w2.shape[3]
-    rgb = w3.shape[3]
+def tap_codes(rows, lanes, rgb, later):
+    row = lax.broadcasted_iota(jnp.int32, (rows, lanes), 0)
+    lane = lax.broadcasted_iota(jnp.int32, (rows, lanes), 1)
+    a, colour, b, time = row % 4, row // 4 % 4, row // 16 % 4, later - row // 64
+    c, e, d, t = lane % rgb, lane // rgb % 3, lane // (3 * rgb) % 3, lane // (9 * rgb)
+    same = (c == colour) & (t == time)
+    return jnp.where(same, a + d, -99), jnp.where(same, b + e, -99)
+
+
+def tap_weights(w3, wc3, w3c, flat):
+    rgb, c3 = w3.shape[3:]
     flat[...] = jnp.zeros_like(flat)
     for t in range(3):
         for d in range(3):
             for e in range(3):
                 row = ((t * 3 + d) * 3 + e) * rgb
-                value = w3[t, d, e].astype(F32)
-                flat[row:row + rgb, 0:c3] = value
-                flat[96 + row:96 + row + rgb, c3:2 * c3] = value
-    three = flat[0:96, 0:128].astype(BF16)
-    w3c[...] = jnp.dot(taps3c[...], three, preferred_element_type=F32).astype(BF16)
-    wc3[:, 0:2 * c3] = jnp.dot(taps3[...], flat[...].astype(BF16), preferred_element_type=F32).astype(BF16)
+                flat[row:row + rgb, 0:c3] = w3[t, d, e].astype(F32)
+    taps = flat[...].astype(BF16)
+    one = lambda cond: jnp.where(cond, 1.0, 0.0).astype(BF16)
+    down, over = tap_codes(128, 128, rgb, 1)
+    code = down * 8 + over
+    for j in range(6):
+        for k in range(6):
+            base = (j * 6 + k) * 128
+            w3c[base:base + 128] = jnp.dot(one(code == j * 8 + k), taps, preferred_element_type=F32).astype(BF16)
+    down, over = tap_codes(192, 128, rgb, 2)
+    code = ((down + 1) // 2) * 8 + (over + 1) // 2
+    lanes = wc3.shape[-1]
+    wc3[:, 2 * c3:lanes] = jnp.zeros((wc3.shape[0], lanes - 2 * c3), BF16)
+    for rs in range(2):
+        for cs in range(4):
+            base = (rs * 4 + cs) * 192
+            for half in range(2):
+                place = {(0, 1): 0, (0, 0): 1, (1, 1): 2, (1, 0): 3}[rs, half]
+                value = jnp.dot(one(code == place * 8 + cs), taps, preferred_element_type=F32)
+                wc3[base:base + 192, half * c3:(half + 1) * c3] = value[:, 0:c3].astype(BF16)
+
+
+def phase_weights(w2, wc2):
+    c3 = w2.shape[3]
     for t in range(3):
         rows = {}
         for e in range(3):
@@ -204,7 +188,19 @@
                     wc2[base, c3:2 * c3, 0:2 * c3] = cols[2 * rs + 1].astype(BF16)
     lanes = wc2.shape[-1]
     wc2[:, :, 2 * c3:lanes] = jnp.zeros(wc2.shape[:2] + (lanes - 2 * c3,), BF16)
-    wc3[:, 2 * c3:lanes] = jnp.zeros((wc3.shape[0], lanes - 2 * c3), BF16)
+
+
+def weights_kernel(w1_hbm, w2_hbm, w3, w1, w2, wc2, wc3, w3c, flat, sems):
+    copies = [
+        pltpu.make_async_copy(src, dst, sems.at[i])
+        for i, (src, dst) in enumerate(((w2_hbm, w2), (w1_hbm, w1)))
+    ]
+    for copy in copies:
+        copy.start()
+    tap_weights(w3, wc3, w3c, flat)
+    copies[0].wait()
+    phase_weights(w2, wc2)
+    copies[1].wait()
 
 
 def history_kernel(
@@ -324,11 +320,20 @@
     return out / (1.0 + jnp.exp(-out))
 
 
-def frames_kernel(
-    count, feats, cache, up1, down1, side_a, side_b, dau, dbu, dad, dbd, w1, g1, g2, g3,
-    part2, part3, wc2, wc3, spread_ref,
-    out,
-    e1, x1, e2, x2, x3,
+def insides(flags, width, chans):
+    cols = lax.broadcasted_iota(jnp.int32, (PITCH, chans), 0)
+    first = 1 - flags[2]
+    last = width + flags[3]
+    inside = (cols >= first) & (cols <= last)
+    at_top = inside & (cols < flags[0] * PITCH)
+    at_bottom = inside & (cols < flags[1] * PITCH)
+    return inside, at_top, at_bottom
+
+
+def first_kernel(
+    count, feats, cache, up1, down1, side_a, side_b, dau, dbu, dad, dbd, w1, g1, g2,
+    x2,
+    e1, x1, e2,
 ):
     flags = position(count)
     top, bottom, left, right = sides(flags)
@@ -336,20 +341,13 @@
     old = cache.shape[0]
     total = frames + old
     c2 = g2.shape[0]
-    c3 = c2 // 2
     read = lambda ref, *ix: ref[ix].astype(F32)
 
     off = 8
-    rows1, rows2 = height + 2, height + 1
+    rows1 = height + 2
     lanes2 = e2.shape[-1]
     always = flags[2] + flags[3] > 0
-
-    cols = lax.broadcasted_iota(jnp.int32, (PITCH, c2), 0)
-    first = 1 - flags[2]
-    last = width + flags[3]
-    inside = (cols >= first) & (cols <= last)
-    at_top = inside & (cols < flags[0] * PITCH)
-    at_bottom = inside & (cols < flags[1] * PITCH)
+    inside, at_top, at_bottom = insides(flags, width, c2)
 
     @pl.when(always)
     def _():
@@ -376,9 +374,6 @@
             for f in range(total):
                 for r in range(height + 4):
                     x1[k, f, r] = e1[f, r, off - 2 + k:off - 2 + k + PITCH, :].astype(BF16)
-
-    @pl.when(always)
-    def _():
         pieces = [
             (t, d, e, slice(i, i + 128))
             for t in range(3) for d in range(3) for e in range(3) for i in range(0, chans, 128)
@@ -408,26 +403,46 @@
                 for r in range(rows1):
                     x2[k, f, r] = e2[f, r, off - 1 + k:off - 1 + k + PITCH, :].astype(BF16)
 
+
+def last_kernel(
+    count, x2, g3, part2, part3, wc2, wc3,
+    out,
+    e2, x3,
+):
+    flags = position(count)
+    frames, rows1 = x2.shape[1:3]
+    height = rows1 - 2
+    width = out.shape[3] // 4
+    c3 = g3.shape[0]
+    c2 = 2 * c3
+    off = 8
+    rows2 = height + 1
+    lanes2 = e2.shape[-1]
+    always = flags[2] + flags[3] > 0
+    inside, at_top, at_bottom = insides(flags, width, c2)
+    e2[:, :, :, c2:lanes2] = jnp.zeros(e2.shape[:3] + (lanes2 - c2,), F32)
+
     @pl.when(always)
     def _():
         lanes = lax.broadcasted_iota(jnp.int32, (PITCH, c2), 1)
         lower = lanes < c3
         gain = jnp.concatenate([g3[...].reshape(1, c3)] * 2, -1)
-        every = ([], [])
-        for t in range(3):
-            count = frames - (2 - t)
-            accs = [None, None]
-            for rs in range(2):
-                for q in range(2):
+        every = []
+        for q in range(2):
+            parts = []
+            for t in range(3):
+                count = frames - (2 - t)
+                acc = None
+                for rs in range(2):
                     lhs = [
                         x2[q + cs, 0:count, rs:rs + rows2].reshape(count * rows2 * PITCH, lanes2)
                         for cs in range(2)
                     ]
                     base = ((t * 2 + q) * 2 + rs) * 2
                     term = dot_nt(jnp.concatenate(lhs, -1), jnp.concatenate([wc2[base], wc2[base + 1]], -1))
-                    accs[q] = term if accs[q] is None else accs[q] + term
-            for q in range(2):
-                every[q].append(accs[q].reshape(count, rows2, PITCH, c2))
+                    acc = term if acc is None else acc + term
+                parts.append(acc.reshape(count, rows2, PITCH, c2))
+            every.append(parts)
         for q in range(2):
             parts = every[q]
             for f in range(frames):
@@ -484,11 +499,15 @@
             value = value.T
             turned.append(jnp.concatenate([value[b * 16:(b + 1) * 16] for b in range(4)], -1))
         turned = jnp.concatenate(turned, 0)
+        row = lax.broadcasted_iota(jnp.int32, (4 * size, 4 * size), 0)
+        lane = lax.broadcasted_iota(jnp.int32, (4 * size, 4 * size), 1)
+        place = row % size * 4 + row // size
+        spread = jnp.where(place == lane, 1.0, 0.0).astype(BF16)
         result = None
         for _ in range(3):
             piece = turned.astype(BF16)
             turned = turned - piece.astype(F32)
-            term = jnp.dot(piece, spread_ref[...], preferred_element_type=F32)
+            term = jnp.dot(piece, spread, preferred_element_type=F32)
             result = term if result is None else result + term
         for f in range(frames):
             for c in range(out.shape[1]):
@@ -511,16 +530,18 @@
     vmem = pl.BlockSpec(memory_space=pltpu.VMEM)
     bf = lambda *shape: jax.ShapeDtypeStruct(shape, BF16)
 
-    def call(kernel, ins, outs, scratch, limit, flops, space=vmem):
-        return pl.pallas_call(
+    def call(kernel, ins, outs, scratch, limit, flops, far=()):
+        fn = pl.pallas_call(
             kernel,
             out_shape=outs,
-            in_specs=[space] * len(ins),
+            in_specs=[pl.BlockSpec(memory_space=pltpu.HBM) if i in far else vmem for i in range(len(ins))],
             out_specs=[vmem] * len(outs),
             scratch_shapes=scratch,
             compiler_params=pltpu.CompilerParams(vmem_limit_bytes=int(limit * 2**20)),
             cost_estimate=pl.CostEstimate(flops=flops, bytes_accessed=2_000_000, transcendentals=0),
-        )(*ins)
+        )
+        ins = [pltpu.with_memory_space_constraint(v, pltpu.HBM) if i in far else v for i, v in enumerate(ins)]
+        return fn(*ins)
 
     side = bf(total * height + old * 2 * height, 2, c1)
     corner = bf(total * 2 + old * 2, 2, c1)
@@ -537,7 +558,7 @@
             pltpu.VMEM((old, 4 * height, 8, c3), BF16),
             pltpu.SemaphoreType.DMA((7,)),
         ],
-        62.9, 100_000_000, pl.BlockSpec(memory_space=pltpu.HBM),
+        8, 100_000_000, range(4),
     )
 
     sent = [swap(packed[cp], count, None, cp) for cp in (0, 1)]
@@ -558,11 +579,21 @@
 
     diagonals = [pick(corners[cp]) for pick in (above, below) for cp in (0, 1)]
     size = height * width
-    wc2, wc3, w3c = call(
-        weights_kernel,
-        (w2, w3, jnp.asarray(fine_taps(rgb), BF16), jnp.asarray(cache_taps(rgb), BF16)),
-        [bf(24, 2 * c3, 256), bf(8 * 192, 256), bf(36 * 128, 128)],
-        [pltpu.VMEM((192, 192), F32)], 16, 500_000_000,
+    w1, w2, wc2, wc3, w3c = call(
+        weights_kernel, (w1, w2, w3),
+        [bf(*w1.shape), bf(*w2.shape), bf(24, 2 * c3, 256), bf(8 * 192, 256), bf(36 * 128, 128)],
+        [pltpu.VMEM((128, 128), F32), pltpu.SemaphoreType.DMA((2,))], 16, 500_000_000, (0, 1),
+    )
+    (x2,) = call(
+        functools.partial(first_kernel, count),
+        (feats, old1, above(rows1), below(rows1), *sent, *diagonals, w1, g1, g2),
+        [bf(3, frames, height + 2, PITCH, 256)],
+        [
+            pltpu.VMEM((total, height + 4, 40, c1), F32),
+            pltpu.VMEM((3, total, height + 4, PITCH, c1), BF16),
+            pltpu.VMEM((frames, height + 2, 40, 256), F32),
+        ],
+        20, 6_000_000_000,
     )
     part2, part3 = call(
         functools.partial(history_kernel, count),
@@ -581,20 +612,14 @@
         22, 4_000_000_000,
     )
     (out,) = call(
-        functools.partial(frames_kernel, count),
-        (
-            feats, old1, above(rows1), below(rows1), *sent, *diagonals, w1, g1, g2, g3,
-            part2, part3, wc2, wc3, jnp.asarray(spread(height, width), BF16),
-        ),
+        functools.partial(last_kernel, count),
+        (x2, g3, part2, part3, wc2, wc3),
         [jax.ShapeDtypeStruct((frames, rgb, 4 * height, 4 * width), F32)],
         [
-            pltpu.VMEM((total, height + 4, 40, c1), F32),
-            pltpu.VMEM((3, total, height + 4, PITCH, c1), BF16),
             pltpu.VMEM((frames, height + 2, 40, 256), F32),
-            pltpu.VMEM((3, frames, height + 2, PITCH, 256), BF16),
             pltpu.VMEM((4, frames, height + 1, width, 256), BF16),
         ],
-        26, 10_000_000_000,
+        16, 4_000_000_000,
     )
     return out[:, :, None]
 

time: 41.4 us -> 39 us (0.942)
  local copies, waits for them, and re-layouts: 2.65 us -> 0.05 us
  Pallas kernels: 19.8 us -> 20.5 us
  waiting for transfers between devices: 4.56 us -> 3.95 us
    unnamed x30 -> x16, local copies, waits for them, and re-layouts: 2.65 us -> 0.05 us
    pallas_call x4 -> x5, Pallas kernels: 19.8 us -> 20.5 us  [call(): return fn(*ins)]
    ppermute x6, waiting for transfers between devices: 4.56 us -> 3.95 us  [swap(): return lax.ppermute(values, 'tile', pairs_of(count, row_pair, col_pair))]
  transfers between devices with their start and end apart: 6 -> 6, of which waited for: 1 -> 1; matrix products, arithmetic and copies ran while one was open for 0% -> 0% of each run, Pallas kernels for 11% -> 15%
where the time goes in v2:
time: 39 us; the launch traced here: 38.7 us
  Pallas kernels  20.5 us (53%)
  starting transfers between devices  13.9 us (36%)
  waiting for transfers between devices  3.95 us (10%)
    pallas_call x5, Pallas kernels, call(): return fn(*ins)  20.5 us
    ppermute x6, starting transfers between devices, swap(): return lax.ppermute(values, 'tile', pairs_of(count, row_pair, col_pair))  13.9 us
    ppermute x6, waiting for transfers between devices, swap(): return lax.ppermute(values, 'tile', pairs_of(count, row_pair, col_pair))  3.95 us
  transfers between devices with their start and end apart: 6, of which 1 were waited for; matrix products, arithmetic and copies ran while one was open for 0% of the time, Pallas kernels for 15%

profile of v2, /device:TPU:0, one launch (start us, length us, event | category | flops | bytes accessed | tf_op | source)
XLA Modules:
  0.0 38.7 jit_solution(11460764231828337506)
XLA Ops:
  0.0 0.0 copy-start.4
  0.0 1.7 %shard_map.100 = (bf16[80,2,384]{2,1,0:T(2,128)(2,1)S(1)}, bf16[80,2,384]{2,1,0:T(2,128)(2,1)S(1)}, bf16[2,2,32,384]{3,2,1,0:T(8,128)(2,1)S(1)}, bf16[6,2,16,384...) custom-call(bf16[4,8,16,384]{3,2,1,0:T(8,128)(2,1)} %bitcast.19, ...), custom_call_target="tpu_custom_call" | custom-call | flops 100000000 | bytes 2000000 | tf_op jit(solution)/shard_map/pallas_call | solution.py:544
  1.7 0.6 %collective-permute-start.1 = (bf16[80,2,384]{2,1,0:T(2,128)(2,1)S(1)}, bf16[80,2,384]{2,1,0:T(2,128)(2,1)S(1)}, u32[]{:S(2)}, u32[]{:S(2)}) collective-permute-start(bf16[80,2,384]{2,1,0:T(2,128)(2,1)S(1)} %get-tuple-element.19), channel_id=1, source_target_pairs={{0,1},{1,0},{2,3},{3,2},{4,5},{5,4},{6,7},{7,6},{8,9},{9,8},{10,11... | collective-permute-start | bytes 368648 | tf_op jit(solution)/shard_map/ppermute | solution.py:38
  2.2 7.5 %collective-permute-start.2 = (bf16[80,2,384]{2,1,0:T(2,128)(2,1)S(1)}, bf16[80,2,384]{2,1,0:T(2,128)(2,1)S(1)}, u32[]{:S(2)}, u32[]{:S(2)}) collective-permute-start(bf16[80,2,384]{2,1,0:T(2,128)(2,1)S(1)} %get-tuple-element.20), channel_id=1, source_target_pairs={{0,15},{1,2},{2,1},{3,3},{4,4},{5,6},{6,5},{7,8},{8,7},{9,10},{10,... | collective-permute-start | bytes 368648 | tf_op jit(solution)/shard_map/ppermute | solution.py:38
  9.8 0.1 collective-permute-start.5
  9.9 0.1 collective-permute-start.3
  10.0 0.0 copy-start
  10.0 0.0 copy-start.1
  10.0 3.0 %collective-permute-start.4 = (bf16[16,2,384]{2,1,0:T(2,128)(2,1)S(1)}, bf16[16,2,384]{2,1,0:T(2,128)(2,1)S(1)}, u32[]{:S(2)}, u32[]{:S(2)}) collective-permute-start(bf16[16,2,384]{2,1,0:T(2,128)(2,1)S(1)} %get-tuple-element.22), channel_id=1, source_target_pairs={{0,7},{1,10},{2,9},{3,3},{4,4},{5,14},{6,13},{7,0},{8,15},{9,2},{1... | collective-permute-start | bytes 73736 | tf_op jit(solution)/shard_map/ppermute | solution.py:38
  13.0 0.0 copy-done.4
  13.0 2.6 %shard_map.101 = (bf16[3,3,3,192,384]{4,3,2,1,0:T(8,128)(2,1)S(1)}, bf16[3,3,3,96,192]{4,3,2,1,0:T(8,128)(2,1)S(1)}, bf16[24,192,256]{2,1,0:T(8,128)(2,1)S(1)}, ...) custom-call(bf16[3,3,3,192,384]{4,3,2,1,0:T(8,128)(2,1)} %w1_hbm.1, bf16[3,3,3,96,192]{4,3,2,1,0:T(8,128)(2,1)} %w2_hbm.1, ...), custom_call_target="tpu_custom_call" | custom-call | flops 500000000 | bytes 2000000 | tf_op jit(solution)/shard_map/pallas_call | solution.py:544
  15.6 0.0 collective-permute-done.3.dau.dad
  15.6 2.7 %collective-permute-start = (bf16[6,2,16,384]{3,2,1,0:T(8,128)(2,1)S(1)}, bf16[6,2,16,384]{3,2,1,0:T(8,128)(2,1)S(1)}, u32[]{:S(2)}, u32[]{:S(2)}) collective-permute-start(bf16[6,2,16,384]{3,2,1,0:T(8,128)(2,1)S(1)} %get-tuple-element.18), channel_id=1, source_target_pairs={{0,8},{1,9},{2,10},{3,11},{4,12},{5,13},{6,14},{7,15},{8,0},{9,1},... | collective-permute-start | bytes 442376 | tf_op jit(solution)/shard_map/ppermute | solution.py:38
  18.3 0.0 collective-permute-done.4.dbu.dbd
  18.3 0.0 collective-permute-done.5.up2.down2
  18.3 0.0 collective-permute-done.1.side_a
  18.3 0.0 collective-permute-done.2.side_b
  18.3 0.0 copy-done
  18.3 0.0 copy-done.1
  18.3 0.0 copy-start.2
  18.3 0.0 copy-start.3
  18.3 0.0 copy-start.5
  18.4 0.0 copy-start.6
  18.4 3.4 %shard_map.103 = (f32[2,2,9,24,192]{4,3,2,1,0:T(8,128)S(1)}, f32[2,128,64]{2,1,0:T(8,128)S(1)}) custom-call(bf16[2,16,32,192]{3,2,1,0:T(8,128)(2,1)S(1)} %bitcast.18, bf16[2,32,64,96]{3,2,1,0:T(8,128)(2,1)S(1)} %bitcast.16, bf16[2,2,32,384]{3,2,1,0:T(8,128)(2,1)S(1)} %collective-permute-done.5.up2.down2, ...), custom_call_target="tpu_custom_call" | custom-call | flops 4000000000 | bytes 2000000 | tf_op jit(solution)/shard_map/pallas_call | solution.py:544
  21.8 3.9 %collective-permute-done.up1.down1 = bf16[6,2,16,384]{3,2,1,0:T(8,128)(2,1)S(1)} collective-permute-done((bf16[6,2,16,384]{3,2,1,0:T(8,128)(2,1)S(1)}, bf16[6,2,16,384]{3,2,1,0:T(8,128)(2,1)S(1)}, u32[]{:S(2)}, u32[]{:S(2)}) %collective-permute-start) | collective-permute-done | bytes 147488 | tf_op jit(solution)/shard_map/ppermute | solution.py:38
  25.7 0.0 copy-done.2
  25.7 0.0 copy-done.3
  25.7 0.0 copy-done.5
  25.7 0.0 copy-done.6
  25.7 0.0 copy-start.7
  25.7 7.3 %shard_map.102.x2 = bf16[3,4,10,24,256]{4,3,2,1,0:T(8,128)(2,1)S(1)} custom-call(bf16[4,8,16,384]{3,2,1,0:T(8,128)(2,1)S(1)} %bitcast.20, bf16[2,8,16,384]{3,2,1,0:T(8,128)(2,1)S(1)} %bitcast.22, bf16[6,2,16,384]{3,2,1,0:T(8,128)(2,1)S(1)} %collective-permute-done.up1.down1, bf16[6,2,16,384]{3,2,1,0:T(8,128)(2,1)S(1)} %collective-permute-done.up1.down1, ...), custom_call_target="tpu_custom_call" | custom-call | flops 6000000000 | bytes 2000000 | tf_op jit(solution)/shard_map/pallas_call | solution.py:544
  33.1 0.0 copy-done.7
  33.1 5.6 %shard_map.104 = f32[4,3,32,64]{3,2,1,0:T(8,128)} custom-call(bf16[3,4,10,24,256]{4,3,2,1,0:T(8,128)(2,1)S(1)} %shard_map.102.x2, f32[96]{0:T(128)S(1)} %copy-done.7, f32[2,2,9,24,192]{4,3,2,1,0:T(8,128)S(1)} %get-tuple-element.27.part2, f32[2,128,64]{2,1,0:T(8,128)S(1)} %get-tuple-element.28.part3, bf16[24,192,256]{2,1,0:T(8,128)(2,1)S(1)} %get-tuple-element.29.wc2, ...), custom_call_target="tpu_custom_call" | custom-call | flops 4000000000 | bytes 2000000 | tf_op jit(solution)/shard_map/pallas_call | solution.py:544
Async XLA Ops:
  0.0 13.0 %copy-start.4 = (bf16[3,3,3,3,96]{4,3,2,1,0:T(4,128)(2,1)S(1)}, bf16[3,3,3,3,96]{4,3,2,1,0:T(4,128)(2,1)}, u32[]{:S(2)}) copy-start(bf16[3,3,3,3,96]{4,3,2,1,0:T(4,128)(2,1)} %w3.1) | copy-start | bytes 46660
  1.7 16.6 %collective-permute-start.1 = (bf16[80,2,384]{2,1,0:T(2,128)(2,1)S(1)}, bf16[80,2,384]{2,1,0:T(2,128)(2,1)S(1)}, u32[]{:S(2)}, u32[]{:S(2)}) collective-permute-start(bf16[80,2,384]{2,1,0:T(2,128)(2,1)S(1)} %get-tuple-element.19), channel_id=1, source_target_pairs={{0,1},{1,0},{2,3},{3,2},{4,5},{5,4},{6,7},{7,6},{8,9},{9,8},{10,11... | collective-permute-start | bytes 368648 | tf_op jit(solution)/shard_map/ppermute | solution.py:38
  2.2 16.1 %collective-permute-start.2 = (bf16[80,2,384]{2,1,0:T(2,128)(2,1)S(1)}, bf16[80,2,384]{2,1,0:T(2,128)(2,1)S(1)}, u32[]{:S(2)}, u32[]{:S(2)}) collective-permute-start(bf16[80,2,384]{2,1,0:T(2,128)(2,1)S(1)} %get-tuple-element.20), channel_id=1, source_target_pairs={{0,15},{1,2},{2,1},{3,3},{4,4},{5,6},{6,5},{7,8},{8,7},{9,10},{10,... | collective-permute-start | bytes 368648 | tf_op jit(solution)/shard_map/ppermute | solution.py:38
  9.8 8.5 %collective-permute-start.5 = (bf16[2,2,32,384]{3,2,1,0:T(8,128)(2,1)S(1)}, bf16[2,2,32,384]{3,2,1,0:T(8,128)(2,1)S(1)}, u32[]{:S(2)}, u32[]{:S(2)}) collective-permute-start(bf16[2,2,32,384]{3,2,1,0:T(8,128)(2,1)S(1)} %get-tuple-element.24), channel_id=1, source_target_pairs={{0,8},{1,9},{2,10},{3,11},{4,12},{5,13},{6,14},{7,15},{8,0},{9,1},... | collective-permute-start | bytes 294920 | tf_op jit(solution)/shard_map/ppermute | solution.py:38
  9.9 5.7 %collective-permute-start.3 = (bf16[16,2,384]{2,1,0:T(2,128)(2,1)S(1)}, bf16[16,2,384]{2,1,0:T(2,128)(2,1)S(1)}, u32[]{:S(2)}, u32[]{:S(2)}) collective-permute-start(bf16[16,2,384]{2,1,0:T(2,128)(2,1)S(1)} %get-tuple-element.21), channel_id=1, source_target_pairs={{0,9},{1,8},{2,11},{3,10},{4,13},{5,12},{6,15},{7,14},{8,1},{9,0},... | collective-permute-start | bytes 73736 | tf_op jit(solution)/shard_map/ppermute | solution.py:38
  10.0 8.3 %copy-start = (bf16[2,96,1,32,64]{1,4,3,2,0:T(8,128)(2,1)S(1)}, bf16[2,96,1,32,64]{1,4,3,2,0:T(8,128)(2,1)}, u32[]{:S(2)}) copy-start(bf16[2,96,1,32,64]{1,4,3,2,0:T(8,128)(2,1)} %param.13) | copy-start | bytes 2359300
  10.0 8.3 %copy-start.1 = (bf16[2,192,1,16,32]{1,4,3,2,0:T(8,128)(2,1)S(1)}, bf16[2,192,1,16,32]{1,4,3,2,0:T(8,128)(2,1)}, u32[]{:S(2)}) copy-start(bf16[2,192,1,16,32]{1,4,3,2,0:T(8,128)(2,1)} %param.12) | copy-start | bytes 1179652
  10.0 8.3 %collective-permute-start.4 = (bf16[16,2,384]{2,1,0:T(2,128)(2,1)S(1)}, bf16[16,2,384]{2,1,0:T(2,128)(2,1)S(1)}, u32[]{:S(2)}, u32[]{:S(2)}) collective-permute-start(bf16[16,2,384]{2,1,0:T(2,128)(2,1)S(1)} %get-tuple-element.22), channel_id=1, source_target_pairs={{0,7},{1,10},{2,9},{3,3},{4,4},{5,14},{6,13},{7,0},{8,15},{9,2},{1... | collective-permute-start | bytes 73736 | tf_op jit(solution)/shard_map/ppermute | solution.py:38
  15.6 10.1 %collective-permute-start = (bf16[6,2,16,384]{3,2,1,0:T(8,128)(2,1)S(1)}, bf16[6,2,16,384]{3,2,1,0:T(8,128)(2,1)S(1)}, u32[]{:S(2)}, u32[]{:S(2)}) collective-permute-start(bf16[6,2,16,384]{3,2,1,0:T(8,128)(2,1)S(1)} %get-tuple-element.18), channel_id=1, source_target_pairs={{0,8},{1,9},{2,10},{3,11},{4,12},{5,13},{6,14},{7,15},{8,0},{9,1},... | collective-permute-start | bytes 442376 | tf_op jit(solution)/shard_map/ppermute | solution.py:38
  18.3 7.4 %copy-start.2 = (bf16[4,384,1,8,16]{1,4,3,2,0:T(8,128)(2,1)S(1)}, bf16[4,384,1,8,16]{1,4,3,2,0:T(8,128)(2,1)}, u32[]{:S(2)}) copy-start(bf16[4,384,1,8,16]{1,4,3,2,0:T(8,128)(2,1)} %param.10) | copy-start | bytes 1179652
  18.3 7.4 %copy-start.3 = (bf16[2,384,1,8,16]{1,4,3,2,0:T(8,128)(2,1)S(1)}, bf16[2,384,1,8,16]{1,4,3,2,0:T(8,128)(2,1)}, u32[]{:S(2)}) copy-start(bf16[2,384,1,8,16]{1,4,3,2,0:T(8,128)(2,1)} %param.11) | copy-start | bytes 589828
  18.3 7.4 %copy-start.5 = (f32[384]{0:T(512)S(1)}, f32[384]{0:T(512)}, u32[]{:S(2)}) copy-start(f32[384]{0:T(512)} %g1.1) | copy-start | bytes 4612
  18.4 7.3 %copy-start.6 = (f32[192]{0:T(256)S(1)}, f32[192]{0:T(256)}, u32[]{:S(2)}) copy-start(f32[192]{0:T(256)} %g2.1) | copy-start | bytes 2308
  25.7 7.4 %copy-start.7 = (f32[96]{0:T(128)S(1)}, f32[96]{0:T(128)}, u32[]{:S(2)}) copy-start(f32[96]{0:T(128)} %g3.1) | copy-start | bytes 1156

commit v3 on v2

--- a/solution.py
+++ b/solution.py
@@ -13,6 +13,7 @@
 F32 = jnp.float32
 BF16 = jnp.bfloat16
 PITCH = 24
+PAIR = 40
 
 
 def partner(index, size, odd):
@@ -203,7 +204,7 @@
     copies[1].wait()
 
 
-def history_kernel(
+def history(
     count, second, third, up2, down2, side_a, side_b, dau, dbu, dad, dbd, w2, w3c,
     part2, part3,
     e_lo, e_hi, e3, xc2, xc3,
@@ -347,7 +348,6 @@
     rows1 = height + 2
     lanes2 = e2.shape[-1]
     always = flags[2] + flags[3] > 0
-    inside, at_top, at_bottom = insides(flags, width, c2)
 
     @pl.when(always)
     def _():
@@ -370,10 +370,13 @@
         for f in range(old, total):
             for r in range(height + 4):
                 e1[f, r] = normed(e1[f, r], gain, chans)
+        ringed = width + 2
         for k in range(3):
             for f in range(total):
-                for r in range(height + 4):
-                    x1[k, f, r] = e1[f, r, off - 2 + k:off - 2 + k + PITCH, :].astype(BF16)
+                for r in range(height + 3):
+                    pair = [e1[f, r + i, off - 2 + k:off - 2 + k + ringed, :] for i in range(2)]
+                    pair.append(jnp.zeros((PAIR - 2 * ringed, chans), F32))
+                    x1[k, f, r % 2, r // 2] = jnp.concatenate(pair, 0).astype(BF16)
         pieces = [
             (t, d, e, slice(i, i + 128))
             for t in range(3) for d in range(3) for e in range(3) for i in range(0, chans, 128)
@@ -384,20 +387,29 @@
             rhs = jnp.concatenate([w1[t, d, e, :, ch] for t, d, e, ch in pieces[i:i + 4]], -1)
             for h in range(2):
                 lhs = [
-                    x1[e, t + h * half:t + h * half + half, d:d + rows1, :, ch].reshape(-1, 128)
+                    x1[e, t + h * half:t + h * half + half, d % 2, d // 2:d // 2 + rows1 // 2, :, ch].reshape(-1, 128)
                     for t, d, e, ch in pieces[i:i + 4]
                 ]
                 term = dot_nt(jnp.concatenate(lhs, -1), rhs)
                 accs[h] = term if accs[h] is None else accs[h] + term
-        accs = [v.reshape(half, rows1, PITCH, c2) for v in accs]
+        accs = [v.reshape(half, rows1 // 2, PAIR, c2) for v in accs]
 
         gain = g2[...].reshape(1, c2)
         e2[:, :, :, c2:lanes2] = jnp.zeros(e2.shape[:3] + (lanes2 - c2,), F32)
+        e2[:, :, 24:e2.shape[2], 0:c2] = jnp.zeros(e2.shape[:2] + (e2.shape[2] - 24, c2), F32)
+        spot = lax.broadcasted_iota(jnp.int32, (PAIR, c2), 0)
+        upper = spot < ringed
+        cols = jnp.where(upper, spot, spot - ringed)
+        within = (cols >= 1 - flags[2]) & (cols <= width + flags[3])
+        top_pair = within & (~upper | (spot < flags[0] * ringed))
+        bottom_pair = within & (upper | (spot < flags[1] * PAIR))
         for f in range(frames):
-            for r in range(rows1):
-                keep = at_top if r == 0 else at_bottom if r == rows1 - 1 else inside
-                value = jnp.where(keep, accs[f // half][f % half, r].astype(BF16).astype(F32), 0.0)
-                e2[f, r, off:off + PITCH, 0:c2] = normed(value, gain, c2)
+            for i in range(rows1 // 2):
+                keep = top_pair if i == 0 else bottom_pair if i == rows1 // 2 - 1 else within
+                value = jnp.where(keep, accs[f // half][f % half, i].astype(BF16).astype(F32), 0.0)
+                value = normed(value, gain, c2)
+                for j in range(2):
+                    e2[f, 2 * i + j, off:off + ringed, 0:c2] = value[j * ringed:(j + 1) * ringed]
         for k in range(3):
             for f in range(frames):
                 for r in range(rows1):
@@ -405,9 +417,9 @@
 
 
 def last_kernel(
-    count, x2, g3, part2, part3, wc2, wc3,
+    count, second, third, up2, down2, side_a, side_b, dau, dbu, dad, dbd, w2, w3c, x2, g3, wc2, wc3,
     out,
-    e2, x3,
+    part2, part3, e_lo, e_hi, e3, xc2, xc3, e2, x3,
 ):
     flags = position(count)
     frames, rows1 = x2.shape[1:3]
@@ -424,6 +436,10 @@
 
     @pl.when(always)
     def _():
+        history(
+            count, second, third, up2, down2, side_a, side_b, dau, dbu, dad, dbd, w2, w3c,
+            part2, part3, e_lo, e_hi, e3, xc2, xc3,
+        )
         lanes = lax.broadcasted_iota(jnp.int32, (PITCH, c2), 1)
         lower = lanes < c3
         gain = jnp.concatenate([g3[...].reshape(1, c3)] * 2, -1)
@@ -431,17 +447,17 @@
         for q in range(2):
             parts = []
             for t in range(3):
-                count = frames - (2 - t)
+                many = frames - (2 - t)
                 acc = None
                 for rs in range(2):
                     lhs = [
-                        x2[q + cs, 0:count, rs:rs + rows2].reshape(count * rows2 * PITCH, lanes2)
+                        x2[q + cs, 0:many, rs:rs + rows2].reshape(many * rows2 * PITCH, lanes2)
                         for cs in range(2)
                     ]
                     base = ((t * 2 + q) * 2 + rs) * 2
                     term = dot_nt(jnp.concatenate(lhs, -1), jnp.concatenate([wc2[base], wc2[base + 1]], -1))
                     acc = term if acc is None else acc + term
-                parts.append(acc.reshape(count, rows2, PITCH, c2))
+                parts.append(acc.reshape(many, rows2, PITCH, c2))
             every.append(parts)
         for q in range(2):
             parts = every[q]
@@ -590,36 +606,27 @@
         [bf(3, frames, height + 2, PITCH, 256)],
         [
             pltpu.VMEM((total, height + 4, 40, c1), F32),
-            pltpu.VMEM((3, total, height + 4, PITCH, c1), BF16),
+            pltpu.VMEM((3, total, 2, height // 2 + 2, PAIR, c1), BF16),
             pltpu.VMEM((frames, height + 2, 40, 256), F32),
         ],
-        20, 6_000_000_000,
+        22, 6_000_000_000,
     )
-    part2, part3 = call(
-        functools.partial(history_kernel, count),
-        (old2, old3, above(rows2), below(rows2), *sent, *diagonals, w2, w3c),
+    (out,) = call(
+        functools.partial(last_kernel, count),
+        (old2, old3, above(rows2), below(rows2), *sent, *diagonals, w2, w3c, x2, g3, wc2, wc3),
+        [jax.ShapeDtypeStruct((frames, rgb, 4 * height, 4 * width), F32)],
         [
-            jax.ShapeDtypeStruct((2, 2, height + 1, PITCH, c2), F32),
-            jax.ShapeDtypeStruct((2, size, 64), F32),
-        ],
-        [
+            pltpu.VMEM((2, 2, height + 1, PITCH, c2), F32),
+            pltpu.VMEM((2, size, 64), F32),
             pltpu.VMEM((old, 2 * height + 4, 64, 128), F32),
             pltpu.VMEM((old, 2 * height + 4, 64, 128), F32),
             pltpu.VMEM((old, 4 * height + 2, 96, 128), F32),
             pltpu.VMEM((4, old, 2 * height + 4, PITCH, c2), BF16),
             pltpu.VMEM((6, old, height + 1, 4, width, 128), BF16),
-        ],
-        22, 4_000_000_000,
-    )
-    (out,) = call(
-        functools.partial(last_kernel, count),
-        (x2, g3, part2, part3, wc2, wc3),
-        [jax.ShapeDtypeStruct((frames, rgb, 4 * height, 4 * width), F32)],
-        [
             pltpu.VMEM((frames, height + 2, 40, 256), F32),
             pltpu.VMEM((4, frames, height + 1, width, 256), BF16),
         ],
-        16, 4_000_000_000,
+        30, 8_000_000_000,
     )
     return out[:, :, None]
 

time: 39 us -> 34.1 us (0.87)
  waiting for transfers between devices: 3.95 us -> 0.02 us
  Pallas kernels: 20.5 us -> 19.4 us
    ppermute x6, waiting for transfers between devices: 3.95 us -> 0.02 us  [swap(): return lax.ppermute(values, 'tile', pairs_of(count, row_pair, col_pair))]
    pallas_call x5 -> x4, Pallas kernels: 20.5 us -> 19.4 us  [call(): return fn(*ins)]
  transfers between devices with their start and end apart: 6 -> 6, of which waited for: 1 -> 0; matrix products, arithmetic and copies ran while one was open for 0% -> 0% of each run, Pallas kernels for 15% -> 27%
where the time goes in v3:
time: 34.1 us; the launch traced here: 33.6 us
  Pallas kernels  19.4 us (57%)
  starting transfers between devices  13.9 us (41%)
    pallas_call x4, Pallas kernels, call(): return fn(*ins)  19.4 us
    ppermute x6, starting transfers between devices, swap(): return lax.ppermute(values, 'tile', pairs_of(count, row_pair, col_pair))  13.9 us
  transfers between devices with their start and end apart: 6, of which 0 were waited for; matrix products, arithmetic and copies ran while one was open for 0% of the time, Pallas kernels for 27%

profile of v3, /device:TPU:0, one launch (start us, length us, event | category | flops | bytes accessed | tf_op | source)
XLA Modules:
  0.0 33.6 jit_solution(13145261135311807743)
XLA Ops:
  0.0 0.0 copy-start.4
  0.0 1.7 %shard_map.100 = (bf16[80,2,384]{2,1,0:T(2,128)(2,1)S(1)}, bf16[80,2,384]{2,1,0:T(2,128)(2,1)S(1)}, bf16[2,2,32,384]{3,2,1,0:T(8,128)(2,1)S(1)}, bf16[6,2,16,384...) custom-call(bf16[4,8,16,384]{3,2,1,0:T(8,128)(2,1)} %bitcast.19, ...), custom_call_target="tpu_custom_call" | custom-call | flops 100000000 | bytes 2000000 | tf_op jit(solution)/shard_map/pallas_call | solution.py:560
  1.7 4.1 %collective-permute-start.5 = (bf16[6,2,16,384]{3,2,1,0:T(8,128)(2,1)S(1)}, bf16[6,2,16,384]{3,2,1,0:T(8,128)(2,1)S(1)}, u32[]{:S(2)}, u32[]{:S(2)}) collective-permute-start(bf16[6,2,16,384]{3,2,1,0:T(8,128)(2,1)S(1)} %get-tuple-element.23), channel_id=1, source_target_pairs={{0,8},{1,9},{2,10},{3,11},{4,12},{5,13},{6,14},{7,15},{8,0},{9,1},... | collective-permute-start | bytes 442376 | tf_op jit(solution)/shard_map/ppermute | solution.py:39
  5.8 0.0 collective-permute-start.1
  5.8 4.3 %collective-permute-start.2 = (bf16[80,2,384]{2,1,0:T(2,128)(2,1)S(1)}, bf16[80,2,384]{2,1,0:T(2,128)(2,1)S(1)}, u32[]{:S(2)}, u32[]{:S(2)}) collective-permute-start(bf16[80,2,384]{2,1,0:T(2,128)(2,1)S(1)} %get-tuple-element.18), channel_id=1, source_target_pairs={{0,15},{1,2},{2,1},{3,3},{4,4},{5,6},{6,5},{7,8},{8,7},{9,10},{10,... | collective-permute-start | bytes 368648 | tf_op jit(solution)/shard_map/ppermute | solution.py:39
  10.1 0.1 collective-permute-start.3
  10.2 0.0 copy-start.2
  10.2 0.0 copy-start.3
  10.2 0.0 copy-start.5
  10.3 0.0 copy-start.6
  10.3 2.8 %collective-permute-start.4 = (bf16[16,2,384]{2,1,0:T(2,128)(2,1)S(1)}, bf16[16,2,384]{2,1,0:T(2,128)(2,1)S(1)}, u32[]{:S(2)}, u32[]{:S(2)}) collective-permute-start(bf16[16,2,384]{2,1,0:T(2,128)(2,1)S(1)} %get-tuple-element.20), channel_id=1, source_target_pairs={{0,7},{1,10},{2,9},{3,3},{4,4},{5,14},{6,13},{7,0},{8,15},{9,2},{1... | collective-permute-start | bytes 73736 | tf_op jit(solution)/shard_map/ppermute | solution.py:39
  13.1 0.0 copy-done.4
  13.1 2.6 %shard_map.101 = (bf16[3,3,3,192,384]{4,3,2,1,0:T(8,128)(2,1)S(1)}, bf16[3,3,3,96,192]{4,3,2,1,0:T(8,128)(2,1)S(1)}, bf16[24,192,256]{2,1,0:T(8,128)(2,1)S(1)}, ...) custom-call(bf16[3,3,3,192,384]{4,3,2,1,0:T(8,128)(2,1)} %w1_hbm.1, bf16[3,3,3,96,192]{4,3,2,1,0:T(8,128)(2,1)} %w2_hbm.1, ...), custom_call_target="tpu_custom_call" | custom-call | flops 500000000 | bytes 2000000 | tf_op jit(solution)/shard_map/pallas_call | solution.py:560
  15.6 0.0 collective-permute-done.3.dau.dad
  15.6 2.7 %collective-permute-start = (bf16[2,2,32,384]{3,2,1,0:T(8,128)(2,1)S(1)}, bf16[2,2,32,384]{3,2,1,0:T(8,128)(2,1)S(1)}, u32[]{:S(2)}, u32[]{:S(2)}) collective-permute-start(bf16[2,2,32,384]{3,2,1,0:T(8,128)(2,1)S(1)} %get-tuple-element.16), channel_id=1, source_target_pairs={{0,8},{1,9},{2,10},{3,11},{4,12},{5,13},{6,14},{7,15},{8,0},{9,1},... | collective-permute-start | bytes 294920 | tf_op jit(solution)/shard_map/ppermute | solution.py:39
  18.3 0.0 collective-permute-done.4.dbu.dbd
  18.3 0.0 collective-permute-done.1.side_a
  18.3 0.0 collective-permute-done.2.side_b
  18.3 0.0 collective-permute-done.5.up1.down1
  18.3 0.0 copy-done.2
  18.3 0.0 copy-done.3
  18.3 0.0 copy-done.5
  18.4 0.0 copy-done.6
  18.4 0.0 copy-start
  18.4 0.0 copy-start.1
  18.4 0.0 copy-start.7
  18.4 6.4 %shard_map.102.x2 = bf16[3,4,10,24,256]{4,3,2,1,0:T(8,128)(2,1)S(1)} custom-call(bf16[4,8,16,384]{3,2,1,0:T(8,128)(2,1)S(1)} %bitcast.20, bf16[2,8,16,384]{3,2,1,0:T(8,128)(2,1)S(1)} %bitcast.22, bf16[6,2,16,384]{3,2,1,0:T(8,128)(2,1)S(1)} %collective-permute-done.5.up1.down1, bf16[6,2,16,384]{3,2,1,0:T(8,128)(2,1)S(1)} %collective-permute-done.5.up1.down1, ...), custom_call_target="tpu_custom_call" | custom-call | flops 6000000000 | bytes 2000000 | tf_op jit(solution)/shard_map/pallas_call | solution.py:560
  24.8 0.0 collective-permute-done.up2.down2
  24.8 0.0 copy-done
  24.8 0.0 copy-done.1
  24.8 0.0 copy-done.7
  24.8 8.8 %shard_map.103 = f32[4,3,32,64]{3,2,1,0:T(8,128)} custom-call(bf16[2,16,32,192]{3,2,1,0:T(8,128)(2,1)S(1)} %bitcast.18, bf16[2,32,64,96]{3,2,1,0:T(8,128)(2,1)S(1)} %bitcast.16, bf16[2,2,32,384]{3,2,1,0:T(8,128)(2,1)S(1)} %collective-permute-done.up2.down2, bf16[2,2,32,384]{3,2,1,0:T(8,128)(2,1)S(1)} %collective-permute-done.up2.down2, ...), custom_call_target="tpu_custom_call" | custom-call | flops 8000000000 | bytes 2000000 | tf_op jit(solution)/shard_map/pallas_call | solution.py:560
Async XLA Ops:
  0.0 13.1 %copy-start.4 = (bf16[3,3,3,3,96]{4,3,2,1,0:T(4,128)(2,1)S(1)}, bf16[3,3,3,3,96]{4,3,2,1,0:T(4,128)(2,1)}, u32[]{:S(2)}) copy-start(bf16[3,3,3,3,96]{4,3,2,1,0:T(4,128)(2,1)} %w3.1) | copy-start | bytes 46660
  1.7 16.6 %collective-permute-start.5 = (bf16[6,2,16,384]{3,2,1,0:T(8,128)(2,1)S(1)}, bf16[6,2,16,384]{3,2,1,0:T(8,128)(2,1)S(1)}, u32[]{:S(2)}, u32[]{:S(2)}) collective-permute-start(bf16[6,2,16,384]{3,2,1,0:T(8,128)(2,1)S(1)} %get-tuple-element.23), channel_id=1, source_target_pairs={{0,8},{1,9},{2,10},{3,11},{4,12},{5,13},{6,14},{7,15},{8,0},{9,1},... | collective-permute-start | bytes 442376 | tf_op jit(solution)/shard_map/ppermute | solution.py:39
  5.8 12.5 %collective-permute-start.1 = (bf16[80,2,384]{2,1,0:T(2,128)(2,1)S(1)}, bf16[80,2,384]{2,1,0:T(2,128)(2,1)S(1)}, u32[]{:S(2)}, u32[]{:S(2)}) collective-permute-start(bf16[80,2,384]{2,1,0:T(2,128)(2,1)S(1)} %get-tuple-element.17), channel_id=1, source_target_pairs={{0,1},{1,0},{2,3},{3,2},{4,5},{5,4},{6,7},{7,6},{8,9},{9,8},{10,11... | collective-permute-start | bytes 368648 | tf_op jit(solution)/shard_map/ppermute | solution.py:39
  5.8 12.5 %collective-permute-start.2 = (bf16[80,2,384]{2,1,0:T(2,128)(2,1)S(1)}, bf16[80,2,384]{2,1,0:T(2,128)(2,1)S(1)}, u32[]{:S(2)}, u32[]{:S(2)}) collective-permute-start(bf16[80,2,384]{2,1,0:T(2,128)(2,1)S(1)} %get-tuple-element.18), channel_id=1, source_target_pairs={{0,15},{1,2},{2,1},{3,3},{4,4},{5,6},{6,5},{7,8},{8,7},{9,10},{10,... | collective-permute-start | bytes 368648 | tf_op jit(solution)/shard_map/ppermute | solution.py:39
  10.1 5.5 %collective-permute-start.3 = (bf16[16,2,384]{2,1,0:T(2,128)(2,1)S(1)}, bf16[16,2,384]{2,1,0:T(2,128)(2,1)S(1)}, u32[]{:S(2)}, u32[]{:S(2)}) collective-permute-start(bf16[16,2,384]{2,1,0:T(2,128)(2,1)S(1)} %get-tuple-element.19), channel_id=1, source_target_pairs={{0,9},{1,8},{2,11},{3,10},{4,13},{5,12},{6,15},{7,14},{8,1},{9,0},... | collective-permute-start | bytes 73736 | tf_op jit(solution)/shard_map/ppermute | solution.py:39
  10.2 8.1 %copy-start.2 = (bf16[4,384,1,8,16]{1,4,3,2,0:T(8,128)(2,1)S(1)}, bf16[4,384,1,8,16]{1,4,3,2,0:T(8,128)(2,1)}, u32[]{:S(2)}) copy-start(bf16[4,384,1,8,16]{1,4,3,2,0:T(8,128)(2,1)} %param.10) | copy-start | bytes 1179652
  10.2 8.1 %copy-start.3 = (bf16[2,384,1,8,16]{1,4,3,2,0:T(8,128)(2,1)S(1)}, bf16[2,384,1,8,16]{1,4,3,2,0:T(8,128)(2,1)}, u32[]{:S(2)}) copy-start(bf16[2,384,1,8,16]{1,4,3,2,0:T(8,128)(2,1)} %param.11) | copy-start | bytes 589828
  10.2 8.1 %copy-start.5 = (f32[384]{0:T(512)S(1)}, f32[384]{0:T(512)}, u32[]{:S(2)}) copy-start(f32[384]{0:T(512)} %g1.1) | copy-start | bytes 4612
  10.3 8.1 %copy-start.6 = (f32[192]{0:T(256)S(1)}, f32[192]{0:T(256)}, u32[]{:S(2)}) copy-start(f32[192]{0:T(256)} %g2.1) | copy-start | bytes 2308
  10.3 8.0 %collective-permute-start.4 = (bf16[16,2,384]{2,1,0:T(2,128)(2,1)S(1)}, bf16[16,2,384]{2,1,0:T(2,128)(2,1)S(1)}, u32[]{:S(2)}, u32[]{:S(2)}) collective-permute-start(bf16[16,2,384]{2,1,0:T(2,128)(2,1)S(1)} %get-tuple-element.20), channel_id=1, source_target_pairs={{0,7},{1,10},{2,9},{3,3},{4,4},{5,14},{6,13},{7,0},{8,15},{9,2},{1... | collective-permute-start | bytes 73736 | tf_op jit(solution)/shard_map/ppermute | solution.py:39
  15.6 9.2 %collective-permute-start = (bf16[2,2,32,384]{3,2,1,0:T(8,128)(2,1)S(1)}, bf16[2,2,32,384]{3,2,1,0:T(8,128)(2,1)S(1)}, u32[]{:S(2)}, u32[]{:S(2)}) collective-permute-start(bf16[2,2,32,384]{3,2,1,0:T(8,128)(2,1)S(1)} %get-tuple-element.16), channel_id=1, source_target_pairs={{0,8},{1,9},{2,10},{3,11},{4,12},{5,13},{6,14},{7,15},{8,0},{9,1},... | collective-permute-start | bytes 294920 | tf_op jit(solution)/shard_map/ppermute | solution.py:39
  18.4 6.5 %copy-start = (bf16[2,96,1,32,64]{1,4,3,2,0:T(8,128)(2,1)S(1)}, bf16[2,96,1,32,64]{1,4,3,2,0:T(8,128)(2,1)}, u32[]{:S(2)}) copy-start(bf16[2,96,1,32,64]{1,4,3,2,0:T(8,128)(2,1)} %param.13) | copy-start | bytes 2359300
  18.4 6.4 %copy-start.1 = (bf16[2,192,1,16,32]{1,4,3,2,0:T(8,128)(2,1)S(1)}, bf16[2,192,1,16,32]{1,4,3,2,0:T(8,128)(2,1)}, u32[]{:S(2)}) copy-start(bf16[2,192,1,16,32]{1,4,3,2,0:T(8,128)(2,1)} %param.12) | copy-start | bytes 1179652
  18.4 6.4 %copy-start.7 = (f32[96]{0:T(128)S(1)}, f32[96]{0:T(128)}, u32[]{:S(2)}) copy-start(f32[96]{0:T(128)} %g3.1) | copy-start | bytes 1156

commit v4 on v3

--- a/solution.py
+++ b/solution.py
@@ -14,6 +14,7 @@
 BF16 = jnp.bfloat16
 PITCH = 24
 PAIR = 40
+TRIPLE = 56
 
 
 def partner(index, size, odd):
@@ -260,7 +261,12 @@
         v0 = acc[0, ..., c3:] + acc[1, ..., :c3]
         v1 = acc[1, ..., c3:]
         for o, v in enumerate((v0, v1)):
-            part2[q, o] = jnp.concatenate([v[:, 1], v[:, 0]], -1)
+            both = jnp.concatenate([v[:, 1], v[:, 0]], -1)
+            ringed = wide // 2 + 2
+            for i in range(part2.shape[2]):
+                rows = [both[3 * i + j, :ringed] for j in range(3)]
+                rows.append(jnp.zeros((TRIPLE - 3 * ringed, 2 * c3), F32))
+                part2[q, o, i] = jnp.concatenate(rows, 0)
 
     tall3, wide3 = third.shape[1:3]
     shift = 2 * 128
@@ -321,16 +327,6 @@
     return out / (1.0 + jnp.exp(-out))
 
 
-def insides(flags, width, chans):
-    cols = lax.broadcasted_iota(jnp.int32, (PITCH, chans), 0)
-    first = 1 - flags[2]
-    last = width + flags[3]
-    inside = (cols >= first) & (cols <= last)
-    at_top = inside & (cols < flags[0] * PITCH)
-    at_bottom = inside & (cols < flags[1] * PITCH)
-    return inside, at_top, at_bottom
-
-
 def first_kernel(
     count, feats, cache, up1, down1, side_a, side_b, dau, dbu, dad, dbd, w1, g1, g2,
     x2,
@@ -412,8 +408,13 @@
                     e2[f, 2 * i + j, off:off + ringed, 0:c2] = value[j * ringed:(j + 1) * ringed]
         for k in range(3):
             for f in range(frames):
-                for r in range(rows1):
-                    x2[k, f, r] = e2[f, r, off - 1 + k:off - 1 + k + PITCH, :].astype(BF16)
+                for rs in range(2):
+                    for i in range(rows1 // 3):
+                        rows = [
+                            e2[f, rs + 3 * i + j, off - 1 + k:off - 1 + k + ringed, :] for j in range(3)
+                        ]
+                        rows.append(jnp.zeros((TRIPLE - 3 * ringed, lanes2), F32))
+                        x2[k, f, rs, i] = jnp.concatenate(rows, 0).astype(BF16)
 
 
 def last_kernel(
@@ -422,8 +423,8 @@
     part2, part3, e_lo, e_hi, e3, xc2, xc3, e2, x3,
 ):
     flags = position(count)
-    frames, rows1 = x2.shape[1:3]
-    height = rows1 - 2
+    frames, _, triples = x2.shape[1:4]
+    height = 3 * triples - 1
     width = out.shape[3] // 4
     c3 = g3.shape[0]
     c2 = 2 * c3
@@ -431,16 +432,16 @@
     rows2 = height + 1
     lanes2 = e2.shape[-1]
     always = flags[2] + flags[3] > 0
-    inside, at_top, at_bottom = insides(flags, width, c2)
     e2[:, :, :, c2:lanes2] = jnp.zeros(e2.shape[:3] + (lanes2 - c2,), F32)
 
     @pl.when(always)
     def _():
-        history(
-            count, second, third, up2, down2, side_a, side_b, dau, dbu, dad, dbd, w2, w3c,
-            part2, part3, e_lo, e_hi, e3, xc2, xc3,
-        )
-        lanes = lax.broadcasted_iota(jnp.int32, (PITCH, c2), 1)
+        ringed = width + 2
+        lanes = lax.broadcasted_iota(jnp.int32, (TRIPLE, c2), 1)
+        spot = lax.broadcasted_iota(jnp.int32, (TRIPLE, c2), 0)
+        row = (spot >= ringed).astype(jnp.int32) + (spot >= 2 * ringed).astype(jnp.int32)
+        cols = spot - row * ringed
+        within = (cols >= 1 - flags[2]) & (cols <= width + flags[3])
         lower = lanes < c3
         gain = jnp.concatenate([g3[...].reshape(1, c3)] * 2, -1)
         every = []
@@ -451,30 +452,32 @@
                 acc = None
                 for rs in range(2):
                     lhs = [
-                        x2[q + cs, 0:many, rs:rs + rows2].reshape(many * rows2 * PITCH, lanes2)
+                        x2[q + cs, 0:many, rs].reshape(many * triples * TRIPLE, lanes2)
                         for cs in range(2)
                     ]
                     base = ((t * 2 + q) * 2 + rs) * 2
                     term = dot_nt(jnp.concatenate(lhs, -1), jnp.concatenate([wc2[base], wc2[base + 1]], -1))
                     acc = term if acc is None else acc + term
-                parts.append(acc.reshape(many, rows2, PITCH, c2))
+                parts.append(acc.reshape(many, triples, TRIPLE, c2))
             every.append(parts)
+        history(
+            count, second, third, up2, down2, side_a, side_b, dau, dbu, dad, dbd, w2, w3c,
+            part2, part3, e_lo, e_hi, e3, xc2, xc3,
+        )
         for q in range(2):
             parts = every[q]
+            top_edge = within & ((row > 0) | lower | (spot < flags[0] * TRIPLE))
+            bottom_edge = within & ((row < 2) | ~lower | (spot < flags[1] * TRIPLE))
             for f in range(frames):
-                for r in range(rows2):
-                    value = parts[2][f, r]
+                for i in range(triples):
+                    value = parts[2][f, i]
                     if f >= 1:
-                        value = value + parts[1][f - 1, r]
+                        value = value + parts[1][f - 1, i]
                     if f >= 2:
-                        value = value + parts[0][f - 2, r]
+                        value = value + parts[0][f - 2, i]
                     else:
-                        value = value + part2[q, f, r]
-                    keep = inside
-                    if r == 0:
-                        keep = (lower & inside) | at_top
-                    if r == rows2 - 1:
-                        keep = (~lower & inside) | at_bottom
+                        value = value + part2[q, f, i]
+                    keep = top_edge if i == 0 else bottom_edge if i == triples - 1 else within
                     value = jnp.where(keep, value.astype(BF16).astype(F32), 0.0)
                     square = value * value
                     sum_low = jnp.sum(jnp.where(lower, square, 0.0), axis=-1, keepdims=True)
@@ -485,7 +488,9 @@
                         lax.rsqrt(sum_high * (1.0 / c3) + EPS),
                     )
                     value = value * scale * gain
-                    e2[f, r, off:off + PITCH, 0:c2] = value / (1.0 + jnp.exp(-value))
+                    value = value / (1.0 + jnp.exp(-value))
+                    for j in range(3):
+                        e2[f, 3 * i + j, off:off + ringed, 0:c2] = value[j * ringed:(j + 1) * ringed]
             for f in range(frames):
                 for r in range(rows2):
                     for cs in ((1, 3) if q == 0 else (0, 2)):
@@ -603,7 +608,7 @@
     (x2,) = call(
         functools.partial(first_kernel, count),
         (feats, old1, above(rows1), below(rows1), *sent, *diagonals, w1, g1, g2),
-        [bf(3, frames, height + 2, PITCH, 256)],
+        [bf(3, frames, 2, (height + 1) // 3, TRIPLE, 256)],
         [
             pltpu.VMEM((total, height + 4, 40, c1), F32),
             pltpu.VMEM((3, total, 2, height // 2 + 2, PAIR, c1), BF16),
@@ -616,7 +621,7 @@
         (old2, old3, above(rows2), below(rows2), *sent, *diagonals, w2, w3c, x2, g3, wc2, wc3),
         [jax.ShapeDtypeStruct((frames, rgb, 4 * height, 4 * width), F32)],
         [
-            pltpu.VMEM((2, 2, height + 1, PITCH, c2), F32),
+            pltpu.VMEM((2, 2, (height + 1) // 3, TRIPLE, c2), F32),
             pltpu.VMEM((2, size, 64), F32),
             pltpu.VMEM((old, 2 * height + 4, 64, 128), F32),
             pltpu.VMEM((old, 2 * height + 4, 64, 128), F32),

time: 34.1 us -> 33.9 us (level)
  no operation moved by 1% of the time
where the time goes in v4:
time: 33.9 us; the launch traced here: 33.4 us
  Pallas kernels  19.2 us (57%)
  starting transfers between devices  13.9 us (41%)
    pallas_call x4, Pallas kernels, call(): return fn(*ins)  19.2 us
    ppermute x6, starting transfers between devices, swap(): return lax.ppermute(values, 'tile', pairs_of(count, row_pair, col_pair))  13.9 us
  transfers between devices with their start and end apart: 6, of which 0 were waited for; matrix products, arithmetic and copies ran while one was open for 0% of the time, Pallas kernels for 27%

profile of v4, /device:TPU:0, one launch (start us, length us, event | category | flops | bytes accessed | tf_op | source)
XLA Modules:
  0.0 33.4 jit_solution(14762088773907588794)
XLA Ops:
  0.0 0.0 copy-start.4
  0.0 1.7 %shard_map.100 = (bf16[80,2,384]{2,1,0:T(2,128)(2,1)S(1)}, bf16[80,2,384]{2,1,0:T(2,128)(2,1)S(1)}, bf16[2,2,32,384]{3,2,1,0:T(8,128)(2,1)S(1)}, bf16[6,2,16,384...) custom-call(bf16[4,8,16,384]{3,2,1,0:T(8,128)(2,1)} %bitcast.19, ...), custom_call_target="tpu_custom_call" | custom-call | flops 100000000 | bytes 2000000 | tf_op jit(solution)/shard_map/pallas_call | solution.py:565
  1.7 4.1 %collective-permute-start.5 = (bf16[6,2,16,384]{3,2,1,0:T(8,128)(2,1)S(1)}, bf16[6,2,16,384]{3,2,1,0:T(8,128)(2,1)S(1)}, u32[]{:S(2)}, u32[]{:S(2)}) collective-permute-start(bf16[6,2,16,384]{3,2,1,0:T(8,128)(2,1)S(1)} %get-tuple-element.23), channel_id=1, source_target_pairs={{0,8},{1,9},{2,10},{3,11},{4,12},{5,13},{6,14},{7,15},{8,0},{9,1},... | collective-permute-start | bytes 442376 | tf_op jit(solution)/shard_map/ppermute | solution.py:40
  5.8 0.0 collective-permute-start.1
  5.8 4.3 %collective-permute-start.2 = (bf16[80,2,384]{2,1,0:T(2,128)(2,1)S(1)}, bf16[80,2,384]{2,1,0:T(2,128)(2,1)S(1)}, u32[]{:S(2)}, u32[]{:S(2)}) collective-permute-start(bf16[80,2,384]{2,1,0:T(2,128)(2,1)S(1)} %get-tuple-element.18), channel_id=1, source_target_pairs={{0,15},{1,2},{2,1},{3,3},{4,4},{5,6},{6,5},{7,8},{8,7},{9,10},{10,... | collective-permute-start | bytes 368648 | tf_op jit(solution)/shard_map/ppermute | solution.py:40
  10.1 0.1 collective-permute-start.3
  10.2 0.0 copy-start.2
  10.2 0.0 copy-start.3
  10.2 0.0 copy-start.5
  10.3 0.0 copy-start.6
  10.3 2.8 %collective-permute-start.4 = (bf16[16,2,384]{2,1,0:T(2,128)(2,1)S(1)}, bf16[16,2,384]{2,1,0:T(2,128)(2,1)S(1)}, u32[]{:S(2)}, u32[]{:S(2)}) collective-permute-start(bf16[16,2,384]{2,1,0:T(2,128)(2,1)S(1)} %get-tuple-element.20), channel_id=1, source_target_pairs={{0,7},{1,10},{2,9},{3,3},{4,4},{5,14},{6,13},{7,0},{8,15},{9,2},{1... | collective-permute-start | bytes 73736 | tf_op jit(solution)/shard_map/ppermute | solution.py:40
  13.1 0.0 copy-done.4
  13.1 2.6 %shard_map.101 = (bf16[3,3,3,192,384]{4,3,2,1,0:T(8,128)(2,1)S(1)}, bf16[3,3,3,96,192]{4,3,2,1,0:T(8,128)(2,1)S(1)}, bf16[24,192,256]{2,1,0:T(8,128)(2,1)S(1)}, ...) custom-call(bf16[3,3,3,192,384]{4,3,2,1,0:T(8,128)(2,1)} %w1_hbm.1, bf16[3,3,3,96,192]{4,3,2,1,0:T(8,128)(2,1)} %w2_hbm.1, ...), custom_call_target="tpu_custom_call" | custom-call | flops 500000000 | bytes 2000000 | tf_op jit(solution)/shard_map/pallas_call | solution.py:565
  15.6 0.0 collective-permute-done.3.dau.dad
  15.6 2.7 %collective-permute-start = (bf16[2,2,32,384]{3,2,1,0:T(8,128)(2,1)S(1)}, bf16[2,2,32,384]{3,2,1,0:T(8,128)(2,1)S(1)}, u32[]{:S(2)}, u32[]{:S(2)}) collective-permute-start(bf16[2,2,32,384]{3,2,1,0:T(8,128)(2,1)S(1)} %get-tuple-element.16), channel_id=1, source_target_pairs={{0,8},{1,9},{2,10},{3,11},{4,12},{5,13},{6,14},{7,15},{8,0},{9,1},... | collective-permute-start | bytes 294920 | tf_op jit(solution)/shard_map/ppermute | solution.py:40
  18.3 0.0 collective-permute-done.4.dbu.dbd
  18.3 0.0 collective-permute-done.1.side_a
  18.3 0.0 collective-permute-done.2.side_b
  18.3 0.0 collective-permute-done.5.up1.down1
  18.3 0.0 copy-done.2
  18.3 0.0 copy-done.3
  18.3 0.0 copy-done.5
  18.4 0.0 copy-done.6
  18.4 0.0 copy-start
  18.4 0.0 copy-start.1
  18.4 0.0 copy-start.7
  18.4 6.6 %shard_map.102.x2 = bf16[3,4,2,3,56,256]{5,4,3,2,1,0:T(8,128)(2,1)S(1)} custom-call(bf16[4,8,16,384]{3,2,1,0:T(8,128)(2,1)S(1)} %bitcast.20, bf16[2,8,16,384]{3,2,1,0:T(8,128)(2,1)S(1)} %bitcast.22, bf16[6,2,16,384]{3,2,1,0:T(8,128)(2,1)S(1)} %collective-permute-done.5.up1.down1, bf16[6,2,16,384]{3,2,1,0:T(8,128)(2,1)S(1)} %collective-permute-done.5.up1.down1, ...), custom_call_target="tpu_custom_call" | custom-call | flops 6000000000 | bytes 2000000 | tf_op jit(solution)/shard_map/pallas_call | solution.py:565
  25.0 0.0 collective-permute-done.up2.down2
  25.0 0.0 copy-done
  25.0 0.0 copy-done.1
  25.0 0.0 copy-done.7
  25.0 8.4 %shard_map.103 = f32[4,3,32,64]{3,2,1,0:T(8,128)} custom-call(bf16[2,16,32,192]{3,2,1,0:T(8,128)(2,1)S(1)} %bitcast.18, bf16[2,32,64,96]{3,2,1,0:T(8,128)(2,1)S(1)} %bitcast.16, bf16[2,2,32,384]{3,2,1,0:T(8,128)(2,1)S(1)} %collective-permute-done.up2.down2, bf16[2,2,32,384]{3,2,1,0:T(8,128)(2,1)S(1)} %collective-permute-done.up2.down2, ...), custom_call_target="tpu_custom_call" | custom-call | flops 8000000000 | bytes 2000000 | tf_op jit(solution)/shard_map/pallas_call | solution.py:565
Async XLA Ops:
  0.0 13.1 %copy-start.4 = (bf16[3,3,3,3,96]{4,3,2,1,0:T(4,128)(2,1)S(1)}, bf16[3,3,3,3,96]{4,3,2,1,0:T(4,128)(2,1)}, u32[]{:S(2)}) copy-start(bf16[3,3,3,3,96]{4,3,2,1,0:T(4,128)(2,1)} %w3.1) | copy-start | bytes 46660
  1.7 16.6 %collective-permute-start.5 = (bf16[6,2,16,384]{3,2,1,0:T(8,128)(2,1)S(1)}, bf16[6,2,16,384]{3,2,1,0:T(8,128)(2,1)S(1)}, u32[]{:S(2)}, u32[]{:S(2)}) collective-permute-start(bf16[6,2,16,384]{3,2,1,0:T(8,128)(2,1)S(1)} %get-tuple-element.23), channel_id=1, source_target_pairs={{0,8},{1,9},{2,10},{3,11},{4,12},{5,13},{6,14},{7,15},{8,0},{9,1},... | collective-permute-start | bytes 442376 | tf_op jit(solution)/shard_map/ppermute | solution.py:40
  5.8 12.5 %collective-permute-start.1 = (bf16[80,2,384]{2,1,0:T(2,128)(2,1)S(1)}, bf16[80,2,384]{2,1,0:T(2,128)(2,1)S(1)}, u32[]{:S(2)}, u32[]{:S(2)}) collective-permute-start(bf16[80,2,384]{2,1,0:T(2,128)(2,1)S(1)} %get-tuple-element.17), channel_id=1, source_target_pairs={{0,1},{1,0},{2,3},{3,2},{4,5},{5,4},{6,7},{7,6},{8,9},{9,8},{10,11... | collective-permute-start | bytes 368648 | tf_op jit(solution)/shard_map/ppermute | solution.py:40
  5.8 12.5 %collective-permute-start.2 = (bf16[80,2,384]{2,1,0:T(2,128)(2,1)S(1)}, bf16[80,2,384]{2,1,0:T(2,128)(2,1)S(1)}, u32[]{:S(2)}, u32[]{:S(2)}) collective-permute-start(bf16[80,2,384]{2,1,0:T(2,128)(2,1)S(1)} %get-tuple-element.18), channel_id=1, source_target_pairs={{0,15},{1,2},{2,1},{3,3},{4,4},{5,6},{6,5},{7,8},{8,7},{9,10},{10,... | collective-permute-start | bytes 368648 | tf_op jit(solution)/shard_map/ppermute | solution.py:40
  10.1 5.5 %collective-permute-start.3 = (bf16[16,2,384]{2,1,0:T(2,128)(2,1)S(1)}, bf16[16,2,384]{2,1,0:T(2,128)(2,1)S(1)}, u32[]{:S(2)}, u32[]{:S(2)}) collective-permute-start(bf16[16,2,384]{2,1,0:T(2,128)(2,1)S(1)} %get-tuple-element.19), channel_id=1, source_target_pairs={{0,9},{1,8},{2,11},{3,10},{4,13},{5,12},{6,15},{7,14},{8,1},{9,0},... | collective-permute-start | bytes 73736 | tf_op jit(solution)/shard_map/ppermute | solution.py:40
  10.2 8.1 %copy-start.2 = (bf16[4,384,1,8,16]{1,4,3,2,0:T(8,128)(2,1)S(1)}, bf16[4,384,1,8,16]{1,4,3,2,0:T(8,128)(2,1)}, u32[]{:S(2)}) copy-start(bf16[4,384,1,8,16]{1,4,3,2,0:T(8,128)(2,1)} %param.10) | copy-start | bytes 1179652
  10.2 8.1 %copy-start.3 = (bf16[2,384,1,8,16]{1,4,3,2,0:T(8,128)(2,1)S(1)}, bf16[2,384,1,8,16]{1,4,3,2,0:T(8,128)(2,1)}, u32[]{:S(2)}) copy-start(bf16[2,384,1,8,16]{1,4,3,2,0:T(8,128)(2,1)} %param.11) | copy-start | bytes 589828
  10.2 8.1 %copy-start.5 = (f32[384]{0:T(512)S(1)}, f32[384]{0:T(512)}, u32[]{:S(2)}) copy-start(f32[384]{0:T(512)} %g1.1) | copy-start | bytes 4612
  10.3 8.1 %copy-start.6 = (f32[192]{0:T(256)S(1)}, f32[192]{0:T(256)}, u32[]{:S(2)}) copy-start(f32[192]{0:T(256)} %g2.1) | copy-start | bytes 2308
  10.3 8.0 %collective-permute-start.4 = (bf16[16,2,384]{2,1,0:T(2,128)(2,1)S(1)}, bf16[16,2,384]{2,1,0:T(2,128)(2,1)S(1)}, u32[]{:S(2)}, u32[]{:S(2)}) collective-permute-start(bf16[16,2,384]{2,1,0:T(2,128)(2,1)S(1)} %get-tuple-element.20), channel_id=1, source_target_pairs={{0,7},{1,10},{2,9},{3,3},{4,4},{5,14},{6,13},{7,0},{8,15},{9,2},{1... | collective-permute-start | bytes 73736 | tf_op jit(solution)/shard_map/ppermute | solution.py:40
  15.6 9.4 %collective-permute-start = (bf16[2,2,32,384]{3,2,1,0:T(8,128)(2,1)S(1)}, bf16[2,2,32,384]{3,2,1,0:T(8,128)(2,1)S(1)}, u32[]{:S(2)}, u32[]{:S(2)}) collective-permute-start(bf16[2,2,32,384]{3,2,1,0:T(8,128)(2,1)S(1)} %get-tuple-element.16), channel_id=1, source_target_pairs={{0,8},{1,9},{2,10},{3,11},{4,12},{5,13},{6,14},{7,15},{8,0},{9,1},... | collective-permute-start | bytes 294920 | tf_op jit(solution)/shard_map/ppermute | solution.py:40
  18.4 6.6 %copy-start = (bf16[2,96,1,32,64]{1,4,3,2,0:T(8,128)(2,1)S(1)}, bf16[2,96,1,32,64]{1,4,3,2,0:T(8,128)(2,1)}, u32[]{:S(2)}) copy-start(bf16[2,96,1,32,64]{1,4,3,2,0:T(8,128)(2,1)} %param.13) | copy-start | bytes 2359300
  18.4 6.6 %copy-start.1 = (bf16[2,192,1,16,32]{1,4,3,2,0:T(8,128)(2,1)S(1)}, bf16[2,192,1,16,32]{1,4,3,2,0:T(8,128)(2,1)}, u32[]{:S(2)}) copy-start(bf16[2,192,1,16,32]{1,4,3,2,0:T(8,128)(2,1)} %param.12) | copy-start | bytes 1179652
  18.4 6.6 %copy-start.7 = (f32[96]{0:T(128)S(1)}, f32[96]{0:T(128)}, u32[]{:S(2)}) copy-start(f32[96]{0:T(128)} %g3.1) | copy-start | bytes 1156
